TPU v7x, 32 devices: a whole 2x2x4 slice. The times are simulated.
32 devices in a mesh: seq: 8 (over z, x), res: 4 (over y, core).
Axes of the slice: x: 2, y: 2, z: 4, core: 2. Of those that a mesh axis runs over, the one named last changes fastest.
Arguments:
- alignment: bfloat16 [128, 256, 256], P('res', 'seq'), may hold values from -6 to 6
- alignment_mask: int32 [128, 256], P('res', 'seq'), may hold values from 0 to 1, as said below
- residue_mask: int32 [256], replicated, may hold values from 0 to 1, as said below
- pair_input: float32 [256, 256, 128], P('seq', 'res'), may hold values from -6 to 6
- outer_gain: float32 [256], replicated, may hold values from 0.25 to 1.75
- left_weight: bfloat16 [256, 32], replicated, may hold values from -0.375 to 0.375
- right_weight: bfloat16 [256, 32], replicated, may hold values from -0.375 to 0.375
- outer_weight: bfloat16 [1024, 128], replicated, may hold values from -1 to 1
- pair_gain: float32 [128], replicated, may hold values from 0.25 to 1.75
- bias_weight: bfloat16 [128, 8], replicated, may hold values from -48 to 48
- row_gain: float32 [256], replicated, may hold values from 0.25 to 1.75
- query_weight: bfloat16 [256, 256], replicated, may hold values from -0.375 to 0.375
- key_weight: bfloat16 [256, 256], replicated, may hold values from -0.375 to 0.375
- value_weight: bfloat16 [256, 256], replicated, may hold values from -0.375 to 0.375
- gate_weight: bfloat16 [256, 256], replicated, may hold values from -0.375 to 0.375
- output_weight: bfloat16 [256, 256], replicated, may hold values from -2 to 2
- transition_gain: float32 [256], replicated, may hold values from 0.25 to 1.75
- up_weight: bfloat16 [256, 1024], replicated, may hold values from -0.375 to 0.375
- down_weight: bfloat16 [1024, 256], replicated, may hold values from -0.1875 to 0.1875
Outputs:
- pair_output: float32 [256, 256, 128], P('seq', 'res')
- alignment_output: float32 [128, 256, 256], P('res', 'seq')
Inputs may be any that keep to these rules, and one draw needn't show every extreme that they name: `residue_mask`: 1 for a present residue, 0 for padding; at least one residue is 1 and at least one is 0. Some residue whose residue_mask is 1 has alignment_mask 1 in every sequence.
All inputs are finite; a program needn't handle non-finite values.
Results may differ from a plain program's by a relative error of at most 0.04.
Values may be sent and summed in bfloat16 or wider, within the bound.
No kernel may reach another device: no remote copies, remote signals or barrier semaphores. Data moves between devices by JAX's collectives and lax.ppermute only.
A program may use at most 128 MiB of HBM per device.

v0:
```python
import math

import jax
import jax.numpy as jnp
from jax import lax
from jax.sharding import PartitionSpec as P

EPSILON = 1e-05
MASKED = -1000000000.0
SCORE_LIMIT = 524288


def layer_norm(values, scales):
    values = values.astype(jnp.float32)
    center = values - jnp.mean(values, -1, keepdims=True)
    spread = jnp.mean(center * center, -1, keepdims=True)
    return center * lax.rsqrt(spread + EPSILON) * scales


def project(values, weight):
    flattened = values.reshape(-1, values.shape[-1])
    result = jnp.dot(flattened, weight, preferred_element_type=jnp.float32)
    return result.reshape(values.shape[:-1] + (weight.shape[1],))


def block_size(length, per_item):
    item_limit = max(1, SCORE_LIMIT // per_item)
    return max(
        (
            divisor
            for divisor in range(1, length + 1)
            if length % divisor == 0 and divisor <= item_limit
        )
    )


def in_blocks(function, arrays, block_rows):
    shaped = tuple(
        (
            member.reshape((member.shape[0] // block_rows, block_rows) + member.shape[1:])
            for member in arrays
        )
    )
    outputs = lax.map(function, shaped)
    return jax.tree.map(lambda member: member.reshape((-1,) + member.shape[2:]), outputs)


def head_scores(query_rows, key_rows, live_keys, head_bias, head_count, score_scale):
    seq_block, row_count, features = query_rows.shape
    key_count = key_rows.shape[1]
    head_size = features // head_count
    scores = jnp.einsum(
        "sihd,sjhd->shij",
        query_rows.reshape(seq_block, row_count, head_count, head_size),
        key_rows.reshape(seq_block, key_count, head_count, head_size),
        preferred_element_type=jnp.float32,
    )
    scores = scores * score_scale + head_bias.astype(jnp.float32)[None]
    return jnp.where(live_keys[:, None, None, :] > 0, scores, MASKED)


def head_weigh(scores, score_peaks, values, head_count):
    weights = jnp.exp(scores - score_peaks[..., None])
    totals = jnp.swapaxes(jnp.sum(weights, -1), 1, 2)
    seq_block, key_count, features = values.shape
    mixed_sum = jnp.einsum(
        "shij,sjhd->sihd",
        weights.astype(jnp.bfloat16),
        values.reshape(seq_block, key_count, head_count, features // head_count),
        preferred_element_type=jnp.float32,
    )
    return (mixed_sum.reshape(seq_block, mixed_sum.shape[1], features), totals)


def on_device(
    alignment,
    alignment_mask,
    residue_mask,
    pair_input,
    outer_gain,
    left_weight,
    right_weight,
    outer_weight,
    pair_gain,
    bias_weight,
    row_gain,
    query_weight,
    key_weight,
    value_weight,
    gate_weight,
    output_weight,
    transition_gain,
    up_weight,
    down_weight,
):
    seq_share, row_count = (alignment.shape[0], alignment.shape[1])
    res_local = pair_input.shape[1]
    seq_total = seq_share * lax.axis_size("res")
    res_total = row_count * lax.axis_size("seq")
    head_count = bias_weight.shape[1]
    outer_width = left_weight.shape[1]
    pair_width = pair_input.shape[2]
    score_scale = (query_weight.shape[1] // head_count) ** (-0.5)
    residue_live = residue_mask.astype(jnp.float32)
    row_live = lax.dynamic_slice_in_dim(residue_live, lax.axis_index("seq") * row_count, row_count)
    column_live = lax.dynamic_slice_in_dim(
        residue_live, lax.axis_index("res") * res_local, res_local
    )
    mask_local = alignment_mask.astype(jnp.bfloat16)
    own_live = alignment_mask.astype(jnp.float32) * row_live[None, :]
    outer_norm = layer_norm(alignment, outer_gain).astype(jnp.bfloat16)
    row_norm = layer_norm(alignment, row_gain).astype(jnp.bfloat16)
    left_local = (project(outer_norm, left_weight) * own_live[..., None]).astype(jnp.bfloat16)
    left_proj, row_mask = (
        lax.all_gather(left_local, "res", axis=0, tiled=True),
        lax.all_gather(mask_local, "res", axis=0, tiled=True),
    )
    row_flags = (row_mask.astype(jnp.float32) * row_live[None, :]).astype(jnp.bfloat16)
    wide_alignment, wide_mask = (
        lax.all_gather(alignment, "seq", axis=1, tiled=True),
        lax.all_gather(mask_local, "seq", axis=1, tiled=True),
    )
    wide_live = wide_mask.astype(jnp.float32) * residue_live[None, :]
    key_norm = layer_norm(wide_alignment, row_gain).astype(jnp.bfloat16)
    outer_wide = layer_norm(wide_alignment, outer_gain).astype(jnp.bfloat16)
    all_keys = project(key_norm, key_weight).astype(jnp.bfloat16)
    all_values = project(key_norm, value_weight).astype(jnp.bfloat16)
    wide_right = (project(outer_wide, right_weight) * wide_live[..., None]).astype(jnp.bfloat16)
    right_proj, column_mask = (
        lax.all_to_all(wide_right, "res", split_axis=1, concat_axis=0, tiled=True),
        lax.all_to_all(wide_mask, "res", split_axis=1, concat_axis=0, tiled=True),
    )
    column_flags = (column_mask.astype(jnp.float32) * column_live[None, :]).astype(jnp.bfloat16)
    right_flat = right_proj.reshape(seq_total, res_local * outer_width)
    row_step = math.gcd(row_count, 16)

    def outer_rows(row_start):
        left_piece = lax.dynamic_slice_in_dim(left_proj, row_start, row_step, 1).reshape(
            seq_total, row_step * outer_width
        )
        product = lax.dot_general(
            left_piece, right_flat, (((0,), (0,)), ((), ())), preferred_element_type=jnp.float32
        )
        product = product.reshape(row_step, outer_width, res_local, outer_width).transpose(
            0, 2, 1, 3
        )
        product = product.reshape(row_step * res_local, outer_width * outer_width).astype(
            jnp.bfloat16
        )
        update = jnp.dot(product, outer_weight, preferred_element_type=jnp.float32).reshape(
            row_step, res_local, pair_width
        )
        live_rows = lax.dynamic_slice_in_dim(row_flags, row_start, row_step, 1)
        counts = lax.dot_general(
            live_rows, column_flags, (((0,), (0,)), ((), ())), preferred_element_type=jnp.float32
        )
        return update / jnp.maximum(counts, 1.0)[..., None]

    starts = jnp.arange(row_count // row_step, dtype=jnp.int32) * row_step
    outer_update = lax.map(outer_rows, starts).reshape(row_count, res_local, pair_width)
    pair_output = pair_input + outer_update
    pair_norm = layer_norm(pair_output, pair_gain).astype(jnp.bfloat16)
    pair_bias = jnp.einsum(
        "ijc,ch->hij", pair_norm, bias_weight, preferred_element_type=jnp.float32
    ).astype(jnp.bfloat16)
    full_bias = lax.all_gather(pair_bias, "res", axis=2, tiled=True)
    own_queries = project(row_norm, query_weight).astype(jnp.bfloat16)
    gate_values = jax.nn.sigmoid(project(row_norm, gate_weight))
    seq_step = block_size(seq_share, head_count * row_count * res_total)

    def attend_piece(members):
        query_piece, key_piece, value_piece, live_piece = members
        scores = head_scores(query_piece, key_piece, live_piece, full_bias, head_count, score_scale)
        return head_weigh(scores, jnp.max(scores, -1), value_piece, head_count)

    mixed_sum, totals = in_blocks(
        attend_piece, (own_queries, all_keys, all_values, wide_live), seq_step
    )
    attended = (
        mixed_sum.reshape(seq_share, row_count, head_count, -1) / totals[..., None]
    ).reshape(seq_share, row_count, -1)
    gated_rows = (attended * gate_values).astype(jnp.bfloat16)
    after_rows = alignment.astype(jnp.float32) + project(gated_rows, output_weight)
    trans_norm = layer_norm(after_rows, transition_gain).astype(jnp.bfloat16)
    hidden_units = jnp.maximum(project(trans_norm, up_weight), 0.0).astype(jnp.bfloat16)
    alignment_output = after_rows + project(hidden_units, down_weight)
    return (pair_output, alignment_output)


def solution(mesh):
    in_specs = (
        P("res", "seq", None),
        P("res", "seq"),
        P(),
        P("seq", "res", None),
        P(),
        P(),
        P(),
        P(),
        P(),
        P(),
        P(),
        P(),
        P(),
        P(),
        P(),
        P(),
        P(),
        P(),
        P(),
    )
    out_specs = (P("seq", "res", None), P("res", "seq", None))
    return jax.shard_map(
        on_device, mesh=mesh, in_specs=in_specs, out_specs=out_specs, check_vma=False
    )
```

profile of v0, /device:TPU:0, one launch (start us, length us, event | category | flops | bytes accessed | tf_op | source)
XLA Modules:
  0.0 229.8 jit_solution(551415257638649572)
XLA Ops:
  8.7 32.9 %all_gather.17 = bf16[32,256]{0,1:T(8,128)(2,1)S(1)} all-gather(bf16[32,32]{0,1:T(8,128)(2,1)S(1)} %convert_element_type.111), channel_id=1, replica_groups=mesh['seq'=8,'res'=4] {'seq'}, dimensions={1}, use_global_device_ids=true | all-gather | bytes 18432 | tf_op jit(solution)/shard_map/all_gather | solution.py:121
  42.4 3.3 %all-to-all-start.1 = ((bf16[4,2,1024]{2,1,0:T(2,128)(2,1)}), bf16[4,2,1024]{2,1,0:T(2,128)(2,1)S(1)}, u32[]{:S(2)}, u32[]{:S(2)}) async-start(bf16[4,2,1024]{2,1,0:T(2,128)(2,1)} %reshape.187), calls=%async_computation.1 | async-start | bytes 32768 | tf_op jit(solution)/shard_map/all_to_all | solution.py:131
  46.6 5.2 %all_gather.18 = bf16[128,32]{1,0:T(8,128)(2,1)S(1)} all-gather(bf16[32,32]{1,0:T(8,128)(2,1)S(1)} %copy.88), channel_id=1, replica_groups=mesh['seq'=8,'res'=4] {'res'}, dimensions={0}, use_global_device_ids=true | all-gather | bytes 10240 | tf_op jit(solution)/shard_map/all_gather | solution.py:116
  52.5 1.3 convert_reduce_fusion.1
  53.7 1.4 fusion.52
  55.9 1.5 fusion.46
  57.5 2.3 %convolution_convert_fusion.2 = bf16[32,32,256]{2,1,0:T(8,128)(2,1)} fusion(bf16[32,32,256]{2,1,0:T(8,128)(2,1)} %param.23, f32[256]{0:T(256)} %param.33, f32[32,32]{1,0:T(8,128)S(1)} %add_rsqrt_fusion.3, f32[32,32]{1,0:T(8,128)S(1)} %broadcast_multiply_fusion.3, bf16[256,256]{1,0:T(8,128)(2,1)} %param.34), kind=kOutput, calls=%fused_computation.56 | convolution fusion | flops 135790592 | bytes 1188864 | tf_op jit(solution)/shard_map/dot_general | solution.py:22
  59.8 10.4 %all_gather.15 = bf16[128,32,32]{2,1,0:T(8,128)(2,1)S(1)} all-gather(bf16[32,32,32]{2,1,0:T(8,128)(2,1)S(1)} %fusion.46), channel_id=1, replica_groups=mesh['seq'=8,'res'=4] {'res'}, dimensions={0}, use_global_device_ids=true | all-gather | bytes 327680 | tf_op jit(solution)/shard_map/all_gather | solution.py:115
  70.3 1.1 copy.90
  71.6 14.5 %all-gather.2.cloned.1.call-done = bf16[32,256,256]{2,1,0:T(8,128)(2,1)} async-done(((bf16[32,32,256]{2,1,0:T(8,128)(2,1)}), bf16[32,256,256]{2,1,0:T(8,128)(2,1)}) %all-gather.2.cloned.1.call-update) | async-done | bytes 4194320 | tf_op jit(solution)/shard_map/all_gather | solution.py:120
  86.0 3.5 %convert_reduce_fusion = f32[32,256]{1,0:T(8,128)S(1)} fusion(bf16[32,256,256]{2,1,0:T(8,128)(2,1)} %all-gather.2.cloned.1.call-done), kind=kLoop, calls=%fused_computation.28 | loop fusion | flops 4186112 | bytes 4227072 | tf_op jit(solution)/shard_map/reduce_sum | solution.py:15
  89.6 2.4 %fusion.23 = f32[32,256]{1,0:T(8,128)S(1)} fusion(bf16[32,256,256]{2,1,0:T(8,128)(2,1)S(1)} %copy-done.1, f32[32,256]{1,0:T(8,128)S(1)} %broadcast_multiply_fusion), kind=kLoop, calls=%fused_computation.35 | loop fusion | flops 8380416 | bytes 4259840 | tf_op jit(solution)/shard_map/reduce_sum | solution.py:16
  92.6 3.7 %fusion.41 = bf16[32,256,32]{1,2,0:T(8,128)(2,1)S(1)} fusion(bf16[32,256,256]{2,1,0:T(8,128)(2,1)S(1)} %copy-done.1, f32[256]{0:T(256)S(1)} %copy-done.20, f32[32,256]{1,0:T(8,128)S(1)} %add_rsqrt_fusion, f32[32,256]{1,0:T(8,128)S(1)} %broadcast_multiply_fusion, f32[32,256]{1,0:T(8,128)S(1)} %get-tuple-element.209, bf16[256,32]{0,1:T(8,128)(2,1)S(1)} %copy-done.19), kind=kOutput, calls=%fused_computation.57 | convolution fusion | flops 145227776 | bytes 4834304 | tf_op jit(solution)/shard_map/dot_general | solution.py:22
  96.4 3.0 %copy.86 = bf16[32,256,32]{2,0,1:T(8,128)(2,1)S(1)} copy(bf16[32,256,32]{1,2,0:T(8,128)(2,1)S(1)} %fusion.41) | data formatting | bytes 1048576 | tf_op jit(solution)/shard_map/convert_element_type | solution.py:128
  99.4 2.9 %reshape.185 = bf16[4,2,32768]{2,1,0:T(2,128)(2,1)} reshape(bf16[256,32,32]{2,1,0:T(8,128)(2,1)S(1)} %bitcast.151) | data formatting | bytes 1048576
  102.3 3.7 %all-to-all-start = ((bf16[4,2,32768]{2,1,0:T(2,128)(2,1)}), bf16[4,2,32768]{2,1,0:T(2,128)(2,1)S(1)}, u32[]{:S(2)}, u32[]{:S(2)}) async-start(bf16[4,2,32768]{2,1,0:T(2,128)(2,1)} %reshape.185), calls=%async_computation | async-start | bytes 1048576 | tf_op jit(solution)/shard_map/all_to_all | solution.py:130
  106.0 5.7 %convolution_convert_fusion.1 = bf16[32,256,256]{2,1,0:T(8,128)(2,1)} fusion(bf16[32,256,256]{2,1,0:T(8,128)(2,1)} %all-gather.2.cloned.1.call-done, f32[256]{0:T(256)} %param.33, f32[32,256]{1,0:T(8,128)} %copy-done.8, f32[32,256]{1,0:T(8,128)S(1)} %broadcast_multiply_fusion, bf16[256,256]{1,0:T(8,128)(2,1)} %param.36), kind=kOutput, calls=%fused_computation.42 | convolution fusion | flops 1086324736 | bytes 8586240 | tf_op jit(solution)/shard_map/dot_general | solution.py:22
  111.8 4.3 %convolution_convert_fusion = bf16[32,256,256]{2,1,0:T(8,128)(2,1)} fusion(bf16[32,256,256]{2,1,0:T(8,128)(2,1)S(1)} %copy-done.2, f32[256]{0:T(256)S(1)} %copy-done.21, f32[32,256]{1,0:T(8,128)S(1)} %copy-done.9, f32[32,256]{1,0:T(8,128)S(1)} %broadcast_multiply_fusion, bf16[256,256]{1,0:T(8,128)(2,1)S(1)} %copy-done.16), kind=kOutput, calls=%fused_computation.41 | convolution fusion | flops 1086324736 | bytes 8586240 | tf_op jit(solution)/shard_map/dot_general | solution.py:22
  116.1 1.1 reshape.186
  117.2 2.2 copy.121
  119.3 3.5 %reshape.165 = bf16[128,2048]{1,0:T(8,128)(2,1)S(1)} reshape(bf16[4,32,64,32]{3,2,1,0:T(8,128)(2,1)} %bitcast.153) | data formatting | bytes 1048576 | tf_op jit(solution)/shard_map/reshape | solution.py:134
  123.2 15.9 %while.22 = (s32[]{:T(128)}, f32[2,16,64,128]{3,2,1,0:T(8,128)}, s32[2]{0:T(128)S(1)}, bf16[128,32,32]{0,2,1:T(8,128)(2,1)S(1)}, bf16[128,2048]{0,1:T(8,128)(2,1...) while((s32[]{:T(128)}, f32[2,16,64,128]{3,2,1,0:T(8,128)}, ...), condition=%wide.region_5.0_spmd, body=%wide.region_4.0_spmd.sunk | while | flops 538313728 | bytes 9863843 | solution.py:160
  125.7 1.3 convert_bitcast_fusion.2
  127.0 1.8 copy.129
  129.0 2.1 fusion.126
  133.6 1.3 convert_bitcast_fusion.2
  134.9 1.8 copy.129
  137.0 2.1 fusion.126
  139.1 1.6 fusion.95
  142.6 7.7 %all_gather.19 = bf16[8,32,256]{1,0,2:T(8,128)(2,1)S(1)} all-gather(bf16[8,32,64]{1,0,2:T(8,128)(2,1)S(1)} %copy.92), channel_id=1, replica_groups=mesh['seq'=8,'res'=4] {'res'}, dimensions={2}, use_global_device_ids=true | all-gather | bytes 163840 | tf_op jit(solution)/shard_map/all_gather | solution.py:166
  150.6 60.1 %while.23 = (s32[]{:T(128)}, f32[4,8,32,256]{3,2,1,0:T(8,128)}, f32[4,8,32,8]{2,3,1,0:T(8,128)S(1)}, bf16[4,8,256,256]{3,2,1,0:T(8,128)(2,1)}, f32[4,8,256]{2,1,...) while((s32[]{:T(128)}, f32[4,8,32,256]{3,2,1,0:T(8,128)}, ...), condition=%wide.region_11.12_spmd, body=%wide.region_8.0_spmd.sunk | while | flops 71366656 | bytes 19509868 | solution.py:44
  150.6 2.7 %constant_dynamic-slice_fusion.5 = (bf16[1,8,256,256]{3,2,1,0:T(8,128)(2,1)S(1)}, bf16[1,8,256,256]{3,2,1,0:T(8,128)(2,1)}) fusion(bf16[4,8,256,256]{3,2,1,0:T(8,128)(2,1)} %get-tuple-element.375, s32[]{:T(128)} %get-tuple-element.360, bf16[4,8,256,256]{3,2,1,0:T(8,128)(2,1)} %get-tuple-element.372), kind=kLoop, calls=%fused_computation.24.clone.1 | loop fusion | bytes 4194308 | tf_op jit(solution)/shard_map/while/body/jit(dynamic_index_in_dim)/dynamic_slice | solution.py:44
  153.2 1.3 copy.132
  154.6 0.9 constant_dynamic-slice_fusion.6
  155.8 1.8 fusion.131
  158.3 2.3 %copy.131 = bf16[1,8,256,256]{2,3,1,0:T(8,128)(2,1)} copy(bf16[1,8,256,256]{3,2,1,0:T(8,128)(2,1)} %get-tuple-element.314) | data formatting | bytes 2097152 | tf_op jit(solution)/shard_map/while/body/jit(dynamic_index_in_dim)/dynamic_slice | solution.py:44
  160.6 2.7 %fusion.132 = f32[8,8,32,32]{3,2,1,0:T(8,128)} fusion(bf16[8,256,8,32]{1,3,2,0:T(8,128)(2,1)} %bitcast.149, f32[8,8,32,256]{3,2,1,0:T(8,128)S(1)} %get-tuple-element.316, f32[8,8,32]{2,1,0:T(8,128)S(1)} %get-tuple-element.317), kind=kOutput, calls=%fused_computation.17.clone.1 | convolution fusion | flops 34603008 | bytes 3416064 | tf_op jit(solution)/shard_map/while/body/eval_jaxpr/shij,sjhd->sihd/dot_general | solution.py:66
  163.3 1.5 copy.133
  165.6 2.7 %constant_dynamic-slice_fusion.5 = (bf16[1,8,256,256]{3,2,1,0:T(8,128)(2,1)S(1)}, bf16[1,8,256,256]{3,2,1,0:T(8,128)(2,1)}) fusion(bf16[4,8,256,256]{3,2,1,0:T(8,128)(2,1)} %get-tuple-element.375, s32[]{:T(128)} %get-tuple-element.360, bf16[4,8,256,256]{3,2,1,0:T(8,128)(2,1)} %get-tuple-element.372), kind=kLoop, calls=%fused_computation.24.clone.1 | loop fusion | bytes 4194308 | tf_op jit(solution)/shard_map/while/body/jit(dynamic_index_in_dim)/dynamic_slice | solution.py:44
  168.3 1.3 copy.132
  169.6 0.9 constant_dynamic-slice_fusion.6
  170.8 1.8 fusion.131
  173.3 2.3 %copy.131 = bf16[1,8,256,256]{2,3,1,0:T(8,128)(2,1)} copy(bf16[1,8,256,256]{3,2,1,0:T(8,128)(2,1)} %get-tuple-element.314) | data formatting | bytes 2097152 | tf_op jit(solution)/shard_map/while/body/jit(dynamic_index_in_dim)/dynamic_slice | solution.py:44
  175.6 2.7 %fusion.132 = f32[8,8,32,32]{3,2,1,0:T(8,128)} fusion(bf16[8,256,8,32]{1,3,2,0:T(8,128)(2,1)} %bitcast.149, f32[8,8,32,256]{3,2,1,0:T(8,128)S(1)} %get-tuple-element.316, f32[8,8,32]{2,1,0:T(8,128)S(1)} %get-tuple-element.317), kind=kOutput, calls=%fused_computation.17.clone.1 | convolution fusion | flops 34603008 | bytes 3416064 | tf_op jit(solution)/shard_map/while/body/eval_jaxpr/shij,sjhd->sihd/dot_general | solution.py:66
  178.4 1.5 copy.133
  180.6 2.7 %constant_dynamic-slice_fusion.5 = (bf16[1,8,256,256]{3,2,1,0:T(8,128)(2,1)S(1)}, bf16[1,8,256,256]{3,2,1,0:T(8,128)(2,1)}) fusion(bf16[4,8,256,256]{3,2,1,0:T(8,128)(2,1)} %get-tuple-element.375, s32[]{:T(128)} %get-tuple-element.360, bf16[4,8,256,256]{3,2,1,0:T(8,128)(2,1)} %get-tuple-element.372), kind=kLoop, calls=%fused_computation.24.clone.1 | loop fusion | bytes 4194308 | tf_op jit(solution)/shard_map/while/body/jit(dynamic_index_in_dim)/dynamic_slice | solution.py:44
  183.3 1.3 copy.132
  184.7 0.9 constant_dynamic-slice_fusion.6
  185.9 1.8 fusion.131
  188.3 2.3 %copy.131 = bf16[1,8,256,256]{2,3,1,0:T(8,128)(2,1)} copy(bf16[1,8,256,256]{3,2,1,0:T(8,128)(2,1)} %get-tuple-element.314) | data formatting | bytes 2097152 | tf_op jit(solution)/shard_map/while/body/jit(dynamic_index_in_dim)/dynamic_slice | solution.py:44
  190.7 2.7 %fusion.132 = f32[8,8,32,32]{3,2,1,0:T(8,128)} fusion(bf16[8,256,8,32]{1,3,2,0:T(8,128)(2,1)} %bitcast.149, f32[8,8,32,256]{3,2,1,0:T(8,128)S(1)} %get-tuple-element.316, f32[8,8,32]{2,1,0:T(8,128)S(1)} %get-tuple-element.317), kind=kOutput, calls=%fused_computation.17.clone.1 | convolution fusion | flops 34603008 | bytes 3416064 | tf_op jit(solution)/shard_map/while/body/eval_jaxpr/shij,sjhd->sihd/dot_general | solution.py:66
  193.4 1.5 copy.133
  195.7 2.7 %constant_dynamic-slice_fusion.5 = (bf16[1,8,256,256]{3,2,1,0:T(8,128)(2,1)S(1)}, bf16[1,8,256,256]{3,2,1,0:T(8,128)(2,1)}) fusion(bf16[4,8,256,256]{3,2,1,0:T(8,128)(2,1)} %get-tuple-element.375, s32[]{:T(128)} %get-tuple-element.360, bf16[4,8,256,256]{3,2,1,0:T(8,128)(2,1)} %get-tuple-element.372), kind=kLoop, calls=%fused_computation.24.clone.1 | loop fusion | bytes 4194308 | tf_op jit(solution)/shard_map/while/body/jit(dynamic_index_in_dim)/dynamic_slice | solution.py:44
  198.3 1.3 copy.132
  199.7 0.9 constant_dynamic-slice_fusion.6
  200.9 1.8 fusion.131
  203.4 2.3 %copy.131 = bf16[1,8,256,256]{2,3,1,0:T(8,128)(2,1)} copy(bf16[1,8,256,256]{3,2,1,0:T(8,128)(2,1)} %get-tuple-element.314) | data formatting | bytes 2097152 | tf_op jit(solution)/shard_map/while/body/jit(dynamic_index_in_dim)/dynamic_slice | solution.py:44
  205.7 2.7 %fusion.132 = f32[8,8,32,32]{3,2,1,0:T(8,128)} fusion(bf16[8,256,8,32]{1,3,2,0:T(8,128)(2,1)} %bitcast.149, f32[8,8,32,256]{3,2,1,0:T(8,128)S(1)} %get-tuple-element.316, f32[8,8,32]{2,1,0:T(8,128)S(1)} %get-tuple-element.317), kind=kOutput, calls=%fused_computation.17.clone.1 | convolution fusion | flops 34603008 | bytes 3416064 | tf_op jit(solution)/shard_map/while/body/eval_jaxpr/shij,sjhd->sihd/dot_general | solution.py:66
  208.4 1.5 copy.133
  210.9 2.6 %div.59 = f32[32,32,8,32]{3,2,1,0:T(8,128)} broadcast(f32[32,32,8]{2,1,0:T(8,128)S(1)} %copy.97), dimensions={0,1,2} | broadcast | bytes 1081344 | tf_op jit(solution)/shard_map/div | solution.py:180
  213.5 3.4 %div.60 = f32[32,32,256]{2,1,0:T(8,128)S(1)} reshape(f32[32,32,8,32]{3,2,1,0:T(8,128)} %div.59) | data formatting | bytes 2097152 | tf_op jit(solution)/shard_map/div | solution.py:180
  216.9 1.1 bitcast_divide_fusion
  218.1 2.0 fusion.97
  220.6 2.4 %fusion.39 = f32[32,32,256]{2,1,0:T(8,128)} fusion(f32[32,32,256]{2,1,0:T(8,128)S(1)} %get-tuple-element.211, bf16[1024,256]{1,0:T(8,128)(2,1)S(1)} %copy-done, bf16[256,1024]{1,0:T(8,128)(2,1)S(1)} %copy-done.14, f32[256]{0:T(256)S(1)} %copy-done.23, f32[32,32]{1,0:T(8,128)S(1)} %add_rsqrt_fusion.1, f32[32,32]{1,0:T(8,128)S(1)} %broadcast_multiply_fusion.2), kind=kOutput, calls=%fused_computation.54 | convolution fusion | flops 1077149696 | bytes 3154944 | tf_op jit(solution)/shard_map/dot_general | solution.py:22
  (115 shorter events, 16.8 us)
Async XLA Ops:
  7.2 213.4 %copy-start = (bf16[1024,256]{1,0:T(8,128)(2,1)S(1)}, bf16[1024,256]{1,0:T(8,128)(2,1)}, u32[]{:S(2)}) copy-start(bf16[1024,256]{1,0:T(8,128)(2,1)} %param.41) | copy-start | bytes 1572868
  7.2 78.9 %all-gather.2.cloned.1.call-start = ((), (), s32[]{:S(2)}) async-start(), calls=%async_computation.2 | async-start | bytes 4718592 | tf_op jit(solution)/shard_map/all_gather | solution.py:120
  42.4 29.0 %all-to-all-start.1 = ((bf16[4,2,1024]{2,1,0:T(2,128)(2,1)}), bf16[4,2,1024]{2,1,0:T(2,128)(2,1)S(1)}, u32[]{:S(2)}, u32[]{:S(2)}) async-start(bf16[4,2,1024]{2,1,0:T(2,128)(2,1)} %reshape.187), calls=%async_computation.1 | async-start | bytes 32768 | tf_op jit(solution)/shard_map/all_to_all | solution.py:131
  55.2 2.3 %copy-start.10 = (f32[32,32]{1,0:T(8,128)}, f32[32,32]{1,0:T(8,128)S(1)}, u32[]{:S(2)}) copy-start(f32[32,32]{1,0:T(8,128)S(1)} %add_rsqrt_fusion.3) | copy-start | bytes 12292
  71.5 21.1 %copy-start.19 = (bf16[256,32]{0,1:T(8,128)(2,1)S(1)}, bf16[256,32]{0,1:T(8,128)(2,1)}, u32[]{:S(2)}) copy-start(bf16[256,32]{0,1:T(8,128)(2,1)} %param.29) | copy-start | bytes 49156
  71.6 21.1 %copy-start.20 = (f32[256]{0:T(256)S(1)}, f32[256]{0:T(256)}, u32[]{:S(2)}) copy-start(f32[256]{0:T(256)} %param.27) | copy-start | bytes 3076
  86.0 3.5 %copy-start.1 = (bf16[32,256,256]{2,1,0:T(8,128)(2,1)S(1)}, bf16[32,256,256]{2,1,0:T(8,128)(2,1)}, u32[]{:S(2)}) copy-start(bf16[32,256,256]{2,1,0:T(8,128)(2,1)} %all-gather.2.cloned.1.call-done) | copy-start | bytes 12582916
  92.0 0.6 copy-start.8
  102.3 13.7 %all-to-all-start = ((bf16[4,2,32768]{2,1,0:T(2,128)(2,1)}), bf16[4,2,32768]{2,1,0:T(2,128)(2,1)S(1)}, u32[]{:S(2)}, u32[]{:S(2)}) async-start(bf16[4,2,32768]{2,1,0:T(2,128)(2,1)} %reshape.185), calls=%async_computation | async-start | bytes 1048576 | tf_op jit(solution)/shard_map/all_to_all | solution.py:130
  106.0 5.8 %copy-start.2 = (bf16[32,256,256]{2,1,0:T(8,128)(2,1)S(1)}, bf16[32,256,256]{2,1,0:T(8,128)(2,1)}, u32[]{:S(2)}) copy-start(bf16[32,256,256]{2,1,0:T(8,128)(2,1)} %all-gather.2.cloned.1.call-done) | copy-start | bytes 12582916
  106.0 5.7 %copy-start.9 = (f32[32,256]{1,0:T(8,128)S(1)}, f32[32,256]{1,0:T(8,128)}, u32[]{:S(2)}) copy-start(f32[32,256]{1,0:T(8,128)} %copy-done.8) | copy-start | bytes 98308
  106.0 5.7 %copy-start.16 = (bf16[256,256]{1,0:T(8,128)(2,1)S(1)}, bf16[256,256]{1,0:T(8,128)(2,1)}, u32[]{:S(2)}) copy-start(bf16[256,256]{1,0:T(8,128)(2,1)} %param.35) | copy-start | bytes 393220
  106.0 5.7 %copy-start.21 = (f32[256]{0:T(256)S(1)}, f32[256]{0:T(256)}, u32[]{:S(2)}) copy-start(f32[256]{0:T(256)} %param.33) | copy-start | bytes 3076
  117.1 6.0 %copy-start.15 = (bf16[1024,128]{1,0:T(8,128)(2,1)S(1)}, bf16[1024,128]{1,0:T(8,128)(2,1)}, u32[]{:S(2)}) copy-start(bf16[1024,128]{1,0:T(8,128)(2,1)} %param.30) | copy-start | bytes 786436
  117.2 6.0 %copy-start.24 = (s32[2]{0:T(128)S(1)}, s32[2]{0:T(128)}, u32[]{:S(2)}) copy-start(s32[2]{0:T(128)} %iota_multiply_fusion) | copy-start | bytes 28
  123.1 15.9 %copy-start.5 = (f32[32,64,128]{2,1,0:T(8,128)S(1)}, f32[32,64,128]{2,1,0:T(8,128)}, u32[]{:S(2)}) copy-start(f32[32,64,128]{2,1,0:T(8,128)} %param.26) | copy-start | bytes 3145732
  139.1 2.6 %copy-start.12 = (bf16[128,8]{0,1:T(8,128)(2,1)S(1)}, bf16[128,8]{0,1:T(8,128)(2,1)}, u32[]{:S(2)}) copy-start(bf16[128,8]{0,1:T(8,128)(2,1)} %param.32) | copy-start | bytes 6148
  139.1 2.6 %copy-start.13 = (f32[128]{0:T(128)S(1)}, f32[128]{0:T(128)}, u32[]{:S(2)}) copy-start(f32[128]{0:T(128)} %param.31) | copy-start | bytes 1540
  139.1 11.5 %copy-start.7 = (f32[4,8,32,8]{2,3,1,0:T(8,128)S(1)}, f32[4,8,32,8]{2,3,1,0:T(8,128)}, u32[]{:S(2)}) copy-start(f32[4,8,32,8]{2,3,1,0:T(8,128)} %custom-call.2) | copy-start | bytes 98308
  140.7 1.0 copy-start.3
  210.9 6.0 %copy-start.6 = (f32[4,8,32,256]{3,2,1,0:T(8,128)S(1)}, f32[4,8,32,256]{3,2,1,0:T(8,128)}, u32[]{:S(2)}) copy-start(f32[4,8,32,256]{3,2,1,0:T(8,128)} %get-tuple-element.88) | copy-start | bytes 3145732
  213.5 4.6 %copy-start.4 = (bf16[32,32,256]{2,1,0:T(8,128)(2,1)S(1)}, bf16[32,32,256]{2,1,0:T(8,128)(2,1)}, u32[]{:S(2)}) copy-start(bf16[32,32,256]{2,1,0:T(8,128)(2,1)} %param.23) | copy-start | bytes 1572868
  213.5 4.6 %copy-start.11 = (f32[32,32]{1,0:T(8,128)S(1)}, f32[32,32]{1,0:T(8,128)}, u32[]{:S(2)}) copy-start(f32[32,32]{1,0:T(8,128)} %copy-done.10) | copy-start | bytes 12292
  213.5 4.6 %copy-start.17 = (bf16[256,256]{1,0:T(8,128)(2,1)S(1)}, bf16[256,256]{1,0:T(8,128)(2,1)}, u32[]{:S(2)}) copy-start(bf16[256,256]{1,0:T(8,128)(2,1)} %param.38) | copy-start | bytes 393220
  213.5 4.6 %copy-start.18 = (bf16[256,256]{1,0:T(8,128)(2,1)S(1)}, bf16[256,256]{1,0:T(8,128)(2,1)}, u32[]{:S(2)}) copy-start(bf16[256,256]{1,0:T(8,128)(2,1)} %param.37) | copy-start | bytes 393220
  213.5 4.6 %copy-start.22 = (f32[256]{0:T(256)S(1)}, f32[256]{0:T(256)}, u32[]{:S(2)}) copy-start(f32[256]{0:T(256)} %param.33) | copy-start | bytes 3076
  218.1 2.4 %copy-start.14 = (bf16[256,1024]{1,0:T(8,128)(2,1)S(1)}, bf16[256,1024]{1,0:T(8,128)(2,1)}, u32[]{:S(2)}) copy-start(bf16[256,1024]{1,0:T(8,128)(2,1)} %param.40) | copy-start | bytes 1572868
  218.1 2.4 %copy-start.23 = (f32[256]{0:T(256)S(1)}, f32[256]{0:T(256)}, u32[]{:S(2)}) copy-start(f32[256]{0:T(256)} %param.39) | copy-start | bytes 3076
Sparse Core Ops, SparseCore 0:
  10.2 75.8 all-gather.1
where the time goes:
time: 231 us; the launch traced here: 230 us
  local copies, waits for them, and re-layouts  67.4 us (29%)
  blocking collectives  56.3 us (24%)
  matrix products  48.2 us (21%)
  other arithmetic  17.2 us (7%)
  waiting for transfers between devices  15.2 us (7%)
  between operations  14.5 us (6%)
  starting transfers between devices  6.94 us (3%)
  loops' own time  4.13 us (2%)
    all_gather x1, blocking collectives, on_device(): lax.all_gather(mask_local, 'seq', axis=1, tiled=True)  32.9 us
    dynamic_slice x16, local copies, waits for them, and re-layouts, in_blocks(): outputs = lax.map(function, shaped)  28.9 us
    dot_general x7, matrix products, project(): result = jnp.dot(flattened, weight, preferred_element_type=jnp.float32)  22 us
    all_gather x1, waiting for transfers between devices, on_device(): lax.all_gather(alignment, 'seq', axis=1, tiled=True)  14.5 us
    dot_general x4, matrix products, head_weigh(): jnp.einsum('shij,sjhd->sihd', weights.astype(jnp.bfloat16), values.reshap...  10.9 us
    all_gather x1, blocking collectives, on_device(): lax.all_gather(left_local, 'res', axis=0, tiled=True)  10.4 us
    dynamic_update_slice x12, local copies, waits for them, and re-layouts, in_blocks(): outputs = lax.map(function, shaped)  9.08 us
    all_gather x1, blocking collectives, on_device(): full_bias = lax.all_gather(pair_bias, 'res', axis=2, tiled=True)  7.68 us
  transfers between devices with their start and end apart: 3, of which 1 were waited for; matrix products, arithmetic and copies ran while one was open for 9% of the time, Pallas kernels for 0%

commit v1 on v0

v1 whole, which is shorter than its diff:
```python
import functools
import math

import jax
import jax.numpy as jnp
from jax import lax
from jax.experimental import pallas as pl
from jax.experimental.pallas import tpu as pltpu
from jax.sharding import PartitionSpec as P


EPSILON = 1e-05
MASKED = -1000000000.0
LANES = 128
ROW_STEP = 256
PACK = 8
VMEM_BYTES = 40 * 1024 * 1024
ALL_VMEM_BYTES = 60 * 1024 * 1024
F32 = jnp.float32
BF16 = jnp.bfloat16


def normalized(values, gain):
    center = values - jnp.mean(values, -1, keepdims=True)
    spread = jnp.mean(center * center, -1, keepdims=True)
    return center * lax.rsqrt(spread + EPSILON) * gain


def dot(left, right, dims=((1,), (0,))):
    return lax.dot_general(left, right, (dims, ((), ())), preferred_element_type=F32)


def where_matrix(shape, test):
    rows = lax.broadcasted_iota(jnp.int32, shape, 0)
    lanes = lax.broadcasted_iota(jnp.int32, shape, 1)
    return jnp.where(test(rows, lanes), 1.0, 0.0).astype(BF16)


def swapped(arrays, axis):
    size = lax.axis_size(axis)
    assert size & (size - 1) == 0
    come = []
    for k, array in enumerate(arrays):
        pairs = [(i, i ^ k) for i in range(size)]
        come.append(lax.ppermute(array, axis, pairs) if k else array)
    return come


def whole(shape):
    return pl.BlockSpec(shape, lambda *_: (0,) * len(shape))


def params(limit=VMEM_BYTES):
    return pltpu.CompilerParams(vmem_limit_bytes=limit)


def factor_kernel(
    sizes,
    x_ref,
    mask_ref,
    residue_ref,
    gain_ref,
    left_w_ref,
    right_w_ref,
    left_ref,
    right_ref,
    norm_ref,
    rows_ref,
):
    seqs, residues, width = sizes
    norm = normalized(x_ref[...].astype(F32), gain_ref[...])
    groups = residues // PACK
    for part in range(norm_ref.shape[0]):
        lanes = slice(part * LANES, (part + 1) * LANES)
        norm_ref[part] = norm[:, lanes]
        for place in range(PACK):
            for group in range(groups):
                at = (place * groups + group) * seqs
                rows_ref[at : at + seqs, lanes] = norm_ref[
                    part, pl.ds(group * PACK + place, seqs, stride=residues), :
                ].astype(BF16)
    span = PACK * width
    spread_left = where_matrix((width, span), lambda r, l: r == l % width)
    spread_right = where_matrix((width, span), lambda r, l: r == l // PACK)
    left_wide = dot(left_w_ref[...], spread_left, ((0,), (0,))).astype(BF16)
    right_wide = dot(right_w_ref[...], spread_right, ((0,), (0,))).astype(BF16)
    rows = rows_ref[...]
    start = lax.axis_index("seq") * residues
    own = where_matrix((residue_ref.shape[1], residues), lambda r, l: r == l + start)
    row_live = dot(residue_ref[...].astype(F32).astype(BF16), own)
    live = (mask_ref[...].astype(F32) * row_live).astype(BF16)
    total = residues * width
    live_left = dot(live, where_matrix((residues, total), lambda r, l: r == l // width))
    live_right = dot(
        live,
        where_matrix((residues, total), lambda r, l: r == (l // span) * PACK + l % PACK),
    )
    live_plain = dot(live, where_matrix((residues, LANES), lambda r, l: r == l)).astype(BF16)
    lane = lax.broadcasted_iota(jnp.int32, (groups * seqs, span), 1)
    for wide, out_refs, live_wide, place_of in (
        (left_wide, [left_ref], live_left, lane // width),
        (
            right_wide,
            [right_ref.at[copy] for copy in range(right_ref.shape[0])],
            live_right,
            lane % PACK,
        ),
    ):
        product = dot(rows, wide)
        packed = product[: groups * seqs]
        for place in range(1, PACK):
            packed = jnp.where(
                place_of == place,
                product[place * groups * seqs : (place + 1) * groups * seqs],
                packed,
            )
        pieces = []
        for group in range(groups):
            piece = packed[group * seqs : (group + 1) * seqs]
            pieces.append((piece * live_wide[:, group * span : (group + 1) * span]).astype(BF16))
        for out_ref in out_refs:
            for group in range(groups):
                out_ref[:, group * span : (group + 1) * span] = pieces[group]
            out_ref[:, total:] = live_plain


def project_kernel(sizes, x_ref, gain_ref, qw_ref, kw_ref, vw_ref, gw_ref, *refs):
    seqs, residues, heads, head, shares, query_scale = sizes
    *sent_refs, gate_ref, rows_ref, qkv_ref = refs
    pack = LANES // head
    groups = seqs // pack
    block = groups * residues
    norm = normalized(x_ref[...].astype(F32), gain_ref[...]).astype(BF16)
    for seq in range(seqs):
        at = (seq % pack) * block + (seq // pack) * residues
        rows_ref[at : at + residues, :] = norm[seq * residues : (seq + 1) * residues]
    features = heads * head
    pair = 2 * LANES
    lane = lax.broadcasted_iota(jnp.int32, (block, pair), 1)
    place_of = (lane % LANES) // head
    own = groups // shares
    for kind, w_ref in enumerate((qw_ref, kw_ref, vw_ref, gw_ref)):
        for two in range(heads // 2):
            base = two * 2 * head
            spread = where_matrix(
                (features, pair),
                lambda r, l: r == base + (l // LANES) * head + l % head,
            )
            wide = dot(w_ref[...], spread).astype(BF16)
            product = dot(rows_ref[...], wide)
            packed = product[:block]
            for place in range(1, pack):
                packed = jnp.where(
                    place_of == place, product[place * block : (place + 1) * block], packed
                )
            if kind == 0:
                packed = packed * query_scale
            if kind == 3:
                packed = jax.nn.sigmoid(packed)
            else:
                packed = packed.astype(BF16)
            for one in range(2):
                for group in range(groups):
                    piece = packed[
                        group * residues : (group + 1) * residues, one * LANES : (one + 1) * LANES
                    ]
                    to = (two * 2 + one) * shares + group // own
                    lanes = slice((group % own) * LANES, (group % own + 1) * LANES)
                    if kind == 3:
                        gate_ref[to, :, lanes] = piece
                    else:
                        qkv_ref[to, kind, :, lanes] = piece
    me = lax.axis_index("seq")
    for offset, sent_ref in enumerate(sent_refs):
        sent_ref[...] = qkv_ref[me ^ offset]


def mask_kernel(sizes, rows_ref, out_ref):
    residues, shares = sizes
    blocks, seqs, _ = rows_ref.shape
    groups, pack, length = out_ref.shape
    live = jnp.zeros((seqs, length), F32)
    for block in range(blocks):
        place = where_matrix((LANES, length), lambda r, l: l == r + block * residues)
        inside = lax.broadcasted_iota(jnp.int32, (LANES, length), 0) < residues
        live = live + dot(rows_ref[block], jnp.where(inside, place, jnp.zeros_like(place)))
    if shares > 1:
        first = (lax.axis_index("seq") % shares) * groups * pack
        chosen = where_matrix((groups * pack, seqs), lambda r, l: l == r + first)
        live = dot(chosen, live.astype(BF16))
    added = (1.0 - live) * MASKED
    for group in range(groups):
        out_ref[group] = added[group * pack : (group + 1) * pack]


def weight_kernel(sizes, outer_w_ref, blocks_ref):
    width, pair_width = sizes
    quad = LANES // width
    blocks_ref[...] = jnp.zeros_like(blocks_ref)
    for e in range(width):
        piece = outer_w_ref[e * width : (e + 1) * width, :]
        for place in range(quad):
            row = e * LANES + place * width
            blocks_ref[row : row + width, place * pair_width : (place + 1) * pair_width] = piece


def widen_kernel(sizes, out_w_ref, wide_ref):
    heads, head = sizes
    spread = where_matrix(
        (heads * LANES, heads * head), lambda r, l: (r // LANES) * head + r % head == l
    )
    wide_ref[...] = dot(spread, out_w_ref[...]).astype(BF16)


def outer_kernel(sizes, right_ref, pair_ref, weight_ref, gain_ref, bias_w_ref, *refs):
    residues, columns, width, pair_width, seqs, shares = sizes
    members = right_ref.shape[0]
    left_refs = refs[:members]
    out_ref, bias_ref, left_ref, stage_ref, norm_ref, bias_rows_ref = refs[members : members + 6]
    held_ref, held_pair_ref, weight_sem, pair_sem = refs[members + 6 :]
    weight_copy = pltpu.make_async_copy(weight_ref, held_ref, weight_sem)
    weight_copy.start()
    pair_copy = pltpu.make_async_copy(pair_ref, held_pair_ref, pair_sem)
    pair_copy.start()
    share = seqs // members
    me = lax.axis_index("res")
    for offset, member_ref in enumerate(left_refs):
        at = pl.multiple_of((me ^ offset) * share, share)
        left_ref[pl.ds(at, share), :] = member_ref[...]
    span = PACK * width
    quad = LANES // width
    groups = residues // quad
    total = residues * width
    blocks = right_ref.shape[1]
    live_left = left_ref[:, total : total + LANES]
    counts = []
    for block in range(blocks):
        live_right = right_ref[:, block, :, total : total + LANES].reshape(seqs, LANES)
        counts.append(dot(live_right.T, live_left)[:residues])
        for two in range(residues // (2 * PACK)):
            flipped = []
            for one in range(2):
                lanes = slice((two * 2 + one) * span, (two * 2 + one + 1) * span)
                flipped.append(right_ref[:, block, :, lanes].reshape(seqs, span).T)
            row = block * residues + two * 2 * PACK
            for chunk in range(total // (2 * LANES)):
                left = left_ref[:, chunk * 2 * LANES : (chunk + 1) * 2 * LANES]
                products = [
                    dot(member, left).reshape(width, PACK, 2 * LANES) for member in flipped
                ]
                joined = jnp.concatenate(products, axis=1).astype(BF16)
                for one in range(2):
                    at = (chunk * 2 + one) * columns + row
                    for e in range(width):
                        stage_ref[at : at + 2 * PACK, e * LANES : (e + 1) * LANES] = joined[
                            e, :, one * LANES : (one + 1) * LANES
                        ]
    scale = 1.0 / jnp.maximum(jnp.concatenate(counts, axis=0), 1.0)
    gain = gain_ref[...]
    weight_copy.wait()
    pair_copy.wait()
    for two in range(quad // 2):
        lanes = slice(two * 2 * pair_width, (two + 1) * 2 * pair_width)
        update = dot(stage_ref[...], held_ref[:, lanes])
        for group in range(groups):
            for one in range(2):
                i = group * quad + two * 2 + one
                piece = update[
                    group * columns : (group + 1) * columns,
                    one * pair_width : (one + 1) * pair_width,
                ]
                value = held_pair_ref[i] + piece * scale[:, i : i + 1]
                out_ref[i] = value
                norm_ref[i] = normalized(value, gain).astype(BF16)
    halves = LANES // columns
    rows = residues // halves
    for row in range(rows):
        joined = jnp.concatenate([norm_ref[row + half * rows] for half in range(halves)], axis=0)
        bias = dot(bias_w_ref[...], joined, ((1,), (1,)))
        for head in range(bias_w_ref.shape[0]):
            bias_rows_ref[head, row : row + 1, :] = bias[head : head + 1, :]
    for to in range(bias_ref.shape[0]):
        piece = bias_rows_ref[to // shares].astype(BF16)
        for other in range(bias_ref.shape[1]):
            bias_ref[to, other] = piece


def attention_kernel(sizes, bias_ref, mask_ref, *refs):
    residues, columns, head, row_step = sizes
    *come_refs, out_ref, full_ref, qkv_ref = refs
    blocks = len(come_refs)
    length = blocks * residues
    me = lax.axis_index("seq")
    for offset, come_ref in enumerate(come_refs):
        at = pl.multiple_of((me ^ offset) * residues, residues)
        for kind in range(3):
            qkv_ref[kind, pl.ds(at, residues), :] = come_ref[kind]
    others = bias_ref.shape[1]
    halves = LANES // columns
    rows = residues // halves

    @pl.when(pl.program_id(0) == 0)
    def _():
        pieces = jnp.concatenate(
            [bias_ref[:, other].reshape(blocks * rows, LANES) for other in range(others)], axis=1
        )
        for half in range(halves):
            place = where_matrix(
                (others * LANES, length),
                lambda r, l: ((r // columns) % halves == half)
                & ((r // LANES) * columns + r % columns == l),
            )
            placed = dot(pieces, place) * math.log2(math.e)
            for block in range(blocks):
                at = block * residues + half * rows
                full_ref[at : at + rows, :] = placed[block * rows : (block + 1) * rows]

    pack = LANES // head
    keys = qkv_ref[1]
    values = qkv_ref[2]
    lane = lax.broadcasted_iota(jnp.int32, (length, LANES), 1) // head
    zeros = jnp.zeros_like(keys)
    ones = jnp.ones_like(keys)
    key_of = [jnp.where(lane == place, keys, zeros) for place in range(pack)]
    value_of = [
        jnp.concatenate(
            [jnp.where(lane == place, values, zeros), jnp.where(lane == place, ones, zeros)], axis=1
        )
        for place in range(pack)
    ]
    value_all = jnp.concatenate(value_of, axis=0)
    per = row_step // residues
    for step in range(length // row_step):
        rows = slice(step * row_step, (step + 1) * row_step)
        queries = qkv_ref[0, rows, :]
        bias = full_ref[rows, :]
        weights = []
        for place in range(pack):
            scores = dot(queries, key_of[place], ((1,), (1,))) + bias + mask_ref[0, place : place + 1]
            weights.append(jnp.exp2(scores - jnp.max(scores, -1, keepdims=True)).astype(BF16))
        both = dot(jnp.concatenate(weights, axis=1), value_all)
        out_ref[step * per : (step + 1) * per] = (
            (both[:, :LANES] / both[:, LANES:]).astype(BF16).reshape(per, residues, LANES)
        )


def finish_kernel(
    sizes, mixed_ref, gate_ref, x_ref, wide_ref, gain_ref, up_ref, down_ref, out_ref
):
    residues, heads, head, _, groups = sizes
    pack = LANES // head
    gated = []
    for group in range(groups):
        lanes = slice(group * LANES, (group + 1) * LANES)
        gated.append(
            jnp.concatenate(
                [
                    (mixed_ref[h, :, lanes].astype(F32) * gate_ref[h, :, lanes]).astype(BF16)
                    for h in range(heads)
                ],
                axis=1,
            )
        )
    gated = jnp.concatenate(gated, axis=0)
    lane = lax.broadcasted_iota(jnp.int32, gated.shape, 1)
    place_of = (lane % LANES) // head
    chosen = jnp.concatenate(
        [jnp.where(place_of == place, gated, jnp.zeros_like(gated)) for place in range(pack)], axis=0
    )
    added = dot(chosen, wide_ref[...])
    order = [group * pack + place for place in range(pack) for group in range(groups)]
    x = jnp.concatenate([x_ref[seq] for seq in order], axis=0).astype(F32)
    after = x + added
    norm = normalized(after, gain_ref[...]).astype(BF16)
    hidden = jnp.maximum(dot(norm, up_ref[...]), 0.0).astype(BF16)
    result = after + dot(hidden, down_ref[...])
    for at, seq in enumerate(order):
        out_ref[seq] = result[at * residues : (at + 1) * residues]


def on_device(
    alignment,
    alignment_mask,
    residue_mask,
    pair_input,
    outer_gain,
    left_weight,
    right_weight,
    outer_weight,
    pair_gain,
    bias_weight,
    row_gain,
    query_weight,
    key_weight,
    value_weight,
    gate_weight,
    output_weight,
    transition_gain,
    up_weight,
    down_weight,
):
    seqs, residues, channels = alignment.shape
    columns, pair_width = pair_input.shape[1:]
    seq_axis, res_axis = lax.axis_size("seq"), lax.axis_size("res")
    heads = bias_weight.shape[1]
    head = query_weight.shape[1] // heads
    width = left_weight.shape[1]
    all_seqs, length = seqs * res_axis, residues * seq_axis
    shares = seq_axis // heads
    own = seqs // shares
    pack = LANES // head
    assert shares * heads == seq_axis and own % pack == 0
    blocks = seq_axis // res_axis
    assert blocks * residues == columns

    flat = alignment.reshape(seqs * residues, channels)
    wide = residues * width + LANES

    left, right = pl.pallas_call(
        functools.partial(factor_kernel, (seqs, residues, width)),
        out_shape=(
            jax.ShapeDtypeStruct((seqs, wide), BF16),
            jax.ShapeDtypeStruct((seq_axis, seqs, wide), BF16),
        ),
        scratch_shapes=[
            pltpu.VMEM((channels // LANES, seqs * residues, LANES), F32),
            pltpu.VMEM((seqs * residues, channels), BF16),
        ],
        compiler_params=params(ALL_VMEM_BYTES),
        cost_estimate=pl.CostEstimate(
            flops=2 * seqs * residues * channels * 2 * PACK * width, bytes_accessed=1 << 20,
            transcendentals=0,
        ),
        name="factors",
    )(flat, alignment_mask, residue_mask[None], outer_gain[None], left_weight.T, right_weight.T)

    right_rows = lax.all_to_all(right, "seq", split_axis=0, concat_axis=0, tiled=True)
    left_all = swapped([left] * res_axis, "res")

    *qkv, gates = pl.pallas_call(
        functools.partial(
            project_kernel,
            (seqs, residues, heads, head, shares, head ** (-0.5) * math.log2(math.e)),
        ),
        out_shape=(
            *(jax.ShapeDtypeStruct((3, residues, own * head), BF16),) * seq_axis,
            jax.ShapeDtypeStruct((seq_axis, residues, own * head), F32),
        ),
        scratch_shapes=[
            pltpu.VMEM((seqs * residues, channels), BF16),
            pltpu.VMEM((seq_axis, 3, residues, own * head), BF16),
        ],
        compiler_params=params(ALL_VMEM_BYTES),
        cost_estimate=pl.CostEstimate(
            flops=2 * seqs * residues * channels * 4 * heads * LANES, bytes_accessed=4 << 20,
            transcendentals=seqs * residues * channels,
        ),
        name="projections",
    )(flat, row_gain[None], query_weight, key_weight, value_weight, gate_weight)

    right_all = lax.all_to_all(right_rows, "res", split_axis=0, concat_axis=0, tiled=True)
    qkv_all = swapped(qkv, "seq")

    mask = pl.pallas_call(
        functools.partial(mask_kernel, (residues, shares)),
        grid=(1,),
        in_specs=[
            pl.BlockSpec((seq_axis, seqs, LANES), lambda _: (0, 0, residues * width // LANES))
        ],
        out_specs=whole((own // pack, pack, length)),
        out_shape=jax.ShapeDtypeStruct((own // pack, pack, length), F32),
        compiler_params=params(),
        cost_estimate=pl.CostEstimate(flops=1 << 26, bytes_accessed=1 << 17, transcendentals=0),
        name="mask",
    )(right_rows)

    flipped_w = outer_weight.reshape(width, width, pair_width).swapaxes(0, 1)
    flipped_w = flipped_w.reshape(width * width, pair_width)
    quad = LANES // width
    wide_outer = pl.pallas_call(
        functools.partial(weight_kernel, (width, pair_width)),
        out_shape=jax.ShapeDtypeStruct((width * LANES, quad * pair_width), BF16),
        compiler_params=params(ALL_VMEM_BYTES),
        cost_estimate=pl.CostEstimate(flops=1 << 29, bytes_accessed=5 << 20, transcendentals=0),
        name="weights",
    )(flipped_w)
    wide_output = pl.pallas_call(
        functools.partial(widen_kernel, (heads, head)),
        out_shape=jax.ShapeDtypeStruct((heads * LANES, channels), BF16),
        compiler_params=params(ALL_VMEM_BYTES),
        cost_estimate=pl.CostEstimate(flops=1 << 28, bytes_accessed=1 << 19, transcendentals=0),
        name="widen",
    )(output_weight)
    halves = LANES // columns
    bias_rows = residues // halves
    pair_output, bias = pl.pallas_call(
        functools.partial(
            outer_kernel, (residues, columns, width, pair_width, all_seqs, shares)
        ),
        in_specs=[
            pl.BlockSpec(memory_space=pl.ANY if at in (1, 2) else pltpu.VMEM)
            for at in range(5 + res_axis)
        ],
        out_shape=(
            jax.ShapeDtypeStruct(pair_input.shape, F32),
            jax.ShapeDtypeStruct((seq_axis, res_axis, bias_rows, LANES), BF16),
        ),
        scratch_shapes=[
            pltpu.VMEM((all_seqs, wide), BF16),
            pltpu.VMEM((residues // quad * columns, width * LANES), BF16),
            pltpu.VMEM((residues, columns, pair_width), BF16),
            pltpu.VMEM((heads, bias_rows, LANES), F32),
            pltpu.VMEM((width * LANES, quad * pair_width), BF16),
            pltpu.VMEM(pair_input.shape, F32),
            pltpu.SemaphoreType.DMA,
            pltpu.SemaphoreType.DMA,
        ],
        compiler_params=params(ALL_VMEM_BYTES),
        cost_estimate=pl.CostEstimate(
            flops=2 * residues * columns * width * width * (all_seqs + 4 * pair_width),
            bytes_accessed=4 << 20,
            transcendentals=0,
        ),
        name="outer",
    )(
        right_all.reshape(res_axis, blocks, seqs, wide),
        pair_input,
        wide_outer,
        pair_gain[None],
        bias_weight.T,
        *left_all,
    )
    bias_all = lax.all_to_all(
        bias.reshape(seq_axis * res_axis, bias_rows, LANES),
        ("seq", "res"),
        split_axis=0,
        concat_axis=0,
        tiled=True,
    ).reshape(seq_axis, res_axis, bias_rows, LANES)

    mixed = pl.pallas_call(
        functools.partial(
            attention_kernel, (residues, columns, head, max(residues, min(length, ROW_STEP)))
        ),
        grid=(own // pack,),
        in_specs=[
            whole((seq_axis, res_axis, bias_rows, LANES)),
            pl.BlockSpec((1, pack, length), lambda g: (g, 0, 0)),
            *(pl.BlockSpec((3, residues, LANES), lambda g: (0, 0, g)),) * seq_axis,
        ],
        out_specs=pl.BlockSpec((seq_axis, residues, LANES), lambda g: (0, 0, g)),
        out_shape=jax.ShapeDtypeStruct((seq_axis, residues, own * head), BF16),
        scratch_shapes=[
            pltpu.VMEM((length, length), F32),
            pltpu.VMEM((3, length, LANES), BF16),
        ],
        compiler_params=params(),
        cost_estimate=pl.CostEstimate(
            flops=4 * own * length * length * LANES, bytes_accessed=2 << 20,
            transcendentals=own * length * length,
        ),
        name="attention",
    )(bias_all, mask, *qkv_all)

    mixed_home = lax.all_to_all(mixed, "seq", split_axis=0, concat_axis=0, tiled=True)

    steps = 2 * shares
    groups = seqs // pack // steps
    per_share = own // pack // groups
    if shares > 1:
        mixed_home = mixed_home.reshape(heads, shares, residues, own * head)
        gates = gates.reshape(heads, shares, residues, own * head)
        share_spec = pl.BlockSpec(
            (heads, None, residues, groups * LANES), lambda g: (0, g // per_share, 0, g % per_share)
        )
    else:
        share_spec = pl.BlockSpec((heads, residues, groups * LANES), lambda g: (0, 0, g))
    hidden = up_weight.shape[1]
    alignment_output = pl.pallas_call(
        functools.partial(finish_kernel, (residues, heads, head, shares, groups)),
        grid=(steps,),
        in_specs=[
            share_spec,
            share_spec,
            pl.BlockSpec((groups * pack, residues, channels), lambda g: (g, 0, 0)),
            whole((heads * LANES, channels)),
            whole((1, channels)),
            whole(up_weight.shape),
            whole(down_weight.shape),
        ],
        out_specs=pl.BlockSpec((groups * pack, residues, channels), lambda g: (g, 0, 0)),
        out_shape=jax.ShapeDtypeStruct(alignment.shape, F32),
        compiler_params=params(),
        cost_estimate=pl.CostEstimate(
            flops=2 * seqs * residues * channels * (4 * channels + 2 * hidden),
            bytes_accessed=4 << 20,
            transcendentals=0,
        ),
        name="finish",
    )(mixed_home, gates, alignment, wide_output, transition_gain[None], up_weight, down_weight)
    return (pair_output, alignment_output)


def solution(mesh):
    spread = P("res", "seq", None)
    pair = P("seq", "res", None)
    in_specs = (spread, P("res", "seq"), P(), pair) + (P(),) * 15

    return jax.shard_map(
        on_device, mesh=mesh, in_specs=in_specs, out_specs=(pair, spread), check_vma=False
    )
```

time: 231 us -> 129 us (0.56)
  local copies, waits for them, and re-layouts: 67.4 us -> 3.95 us
  matrix products: 48.2 us -> 0 us
  Pallas kernels: 0 us -> 34.6 us
  blocking collectives: 56.3 us -> 23.9 us
  starting transfers between devices: 6.94 us -> 31.8 us
  waiting for transfers between devices: 15.2 us -> 33.4 us
  other arithmetic: 17.2 us -> 0 us
  between operations: 14.5 us -> 0.8 us
  loops' own time: 4.13 us -> 0 us
    all_gather x4 -> x0, blocking collectives: 56.3 us -> none  [the longest x1 32.9 us: on_device(): lax.all_gather(mask_local, 'seq', axis=1, tiled=True)]
    dot_general x22 -> x0, matrix products: 48.2 us -> none  [the longest x7 22 us: project(): result = jnp.dot(flattened, weight, preferred_element_type=jnp.float32)]
    pallas_call x0 -> x8, Pallas kernels: none -> 34.6 us  [the longest x1 7.59 us: on_device(): pl.pallas_call(functools.partial(outer_kernel, (residues, columns, width,...]
    dynamic_slice x20 -> x0, local copies, waits for them, and re-layouts: 30.3 us -> none  [the longest x16 28.9 us: in_blocks(): outputs = lax.map(function, shaped)]
    all_to_all x0 -> x1, blocking collectives: none -> 23.9 us  [on_device(): lax.all_to_all(right, 'seq', split_axis=0, concat_axis=0, tiled=True)]
    ppermute x0 -> x10, waiting for transfers between devices: none -> 21.6 us  [swapped(): come.append(lax.ppermute(array, axis, pairs) if k else array)]
    all_gather x1 -> x0, waiting for transfers between devices: 14.5 us -> none  [on_device(): lax.all_gather(alignment, 'seq', axis=1, tiled=True)]
    reduce_sum x11 -> x0, other arithmetic: 13.8 us -> none  [the longest x3 6.36 us: layer_norm(): center = values - jnp.mean(values, -1, keepdims=True)]
  transfers between devices with their start and end apart: 3 -> 13, of which waited for: 1 -> 4; matrix products, arithmetic and copies ran while one was open for 9% -> 1% of each run, Pallas kernels for 0% -> 16%
where the time goes in v1:
time: 129 us; the launch traced here: 128 us
  Pallas kernels  34.6 us (27%)
  waiting for transfers between devices  33.4 us (26%)
  starting transfers between devices  31.8 us (25%)
  blocking collectives  23.9 us (19%)
  local copies, waits for them, and re-layouts  3.95 us (3%)
    all_to_all x1, blocking collectives, on_device(): lax.all_to_all(right, 'seq', split_axis=0, concat_axis=0, tiled=True)  23.9 us
    ppermute x10, waiting for transfers between devices, swapped(): come.append(lax.ppermute(array, axis, pairs) if k else array)  21.6 us
    ppermute x10, starting transfers between devices, swapped(): come.append(lax.ppermute(array, axis, pairs) if k else array)  13.7 us
    all_to_all x1, waiting for transfers between devices, on_device(): lax.all_to_all(mixed, 'seq', split_axis=0, concat_axis=0, tiled=True)  11.8 us
    all_to_all x1, starting transfers between devices, on_device(): lax.all_to_all(mixed, 'seq', split_axis=0, concat_axis=0, tiled=True)  10.7 us
    pallas_call x1, Pallas kernels, on_device(): pl.pallas_call(functools.partial(outer_kernel, (residues, columns, width,...  7.59 us
    pallas_call x1, Pallas kernels, on_device(): pl.pallas_call(functools.partial(attention_kernel, (residues, columns, he...  7.07 us
    pallas_call x1, Pallas kernels, on_device(): pl.pallas_call(functools.partial(project_kernel, (seqs, residues, heads,...  6.54 us
  transfers between devices with their start and end apart: 13, of which 4 were waited for; matrix products, arithmetic and copies ran while one was open for 1% of the time, Pallas kernels for 16%

profile of v1, /device:TPU:0, one launch (start us, length us, event | category | flops | bytes accessed | tf_op | source)
XLA Modules:
  0.0 128.4 jit_solution(11771565229704588526)
XLA Ops:
  0.6 3.4 %factors.1 = (bf16[32,1152]{1,0:T(8,128)(2,1)}, bf16[8,32,1152]{2,1,0:T(8,128)(2,1)}) custom-call(bf16[1024,256]{1,0:T(8,128)(2,1)} %bitcast.17, s32[32,32]{1,0:T(8,128)} %mask_ref.1, s32[1,256]{1,0:T(1,128)} %bitcast.27, f32[1,256]{1,0:T(1,128)} %bitcast.28, bf16[32,256]{1,0:T(8,128)(2,1)} %bitcast.24, bf16[32,256]{1,0:T(8,128)(2,1)} %bitcast.25), custom_call_target="tpu_custom_call" | custom-call | flops 268435456 | bytes 1048576 | tf_op jit(solution)/shard_map/factors/pallas_call | solution.py:419
  4.0 23.9 %all_to_all.20.rows_ref = bf16[8,32,1152]{2,1,0:T(8,128)(2,1)} all-to-all(bf16[8,32,1152]{2,1,0:T(8,128)(2,1)} %get-tuple-element.15), channel_id=1, replica_groups=mesh['seq'=8,'res'=4] {'seq'}, dimensions={0} | all-to-all | bytes 1179648 | tf_op jit(solution)/shard_map/all_to_all | solution.py:437
  27.9 3.5 %all-to-all-start.1 = ((bf16[8,32,1152]{2,1,0:T(8,128)(2,1)}), bf16[8,32,1152]{2,1,0:T(8,128)(2,1)S(1)}, u32[]{:S(2)}, u32[]{:S(2)}) async-start(bf16[8,32,1152]{2,1,0:T(8,128)(2,1)} %all_to_all.20.rows_ref), calls=%async_computation.1 | async-start | bytes 1179648 | tf_op jit(solution)/shard_map/all_to_all | solution.py:461
  31.4 0.0 copy-start.8
  31.4 0.5 collective-permute-start
  31.9 1.6 %collective-permute-start.1 = (bf16[32,1152]{1,0:T(8,128)(2,1)}, bf16[32,1152]{1,0:T(8,128)(2,1)S(1)}, u32[]{:S(2)}, u32[]{:S(2)}) collective-permute-start(bf16[32,1152]{1,0:T(8,128)(2,1)} %get-tuple-element.16.refs_0_), channel_id=1, source_target_pairs={{0,2},{1,3},{2,0},{3,1},{4,6},{5,7},{6,4},{7,5},{8,10},{9,11},{10,... | collective-permute-start | bytes 221192 | tf_op jit(solution)/shard_map/ppermute | solution.py:45
  33.5 0.0 collective-permute-start.2
  33.5 6.5 %projections.1 = (bf16[3,32,1024]{2,1,0:T(8,128)(2,1)}, bf16[3,32,1024]{2,1,0:T(8,128)(2,1)}, bf16[3,32,1024]{2,1,0:T(8,128)(2,1)}, bf16[3,32,1024]{2,1,0:T(8,12...) custom-call(bf16[1024,256]{1,0:T(8,128)(2,1)} %bitcast.18, ...), custom_call_target="tpu_custom_call" | custom-call | flops 2147483648 | bytes 4194304 | tf_op jit(solution)/shard_map/projections/pallas_call | solution.py:440
  40.0 0.8 collective-permute-start.3
  40.9 0.4 collective-permute-start.4
  41.3 0.0 copy-done.8
  41.3 0.8 copy.21
  42.1 3.3 %weights.1.weight_ref = bf16[4096,512]{1,0:T(8,128)(2,1)} custom-call(bf16[1024,128]{1,0:T(8,128)(2,1)} %bitcast.20), custom_call_target="tpu_custom_call" | custom-call | flops 536870912 | bytes 5242880 | tf_op jit(solution)/shard_map/weights/pallas_call | solution.py:480
  45.4 0.0 collective-permute-done.refs_1_
  45.4 0.0 copy-start.10
  45.4 0.0 collective-permute-done.1.refs_2_
  45.4 0.0 copy-start.11
  45.4 0.0 collective-permute-done.2.refs_3_
  45.4 0.0 copy-start.12
  45.4 0.0 all-to-all-done.1
  45.4 0.0 copy-start.7
  45.4 0.6 copy-done.10
  46.0 0.0 copy-done.11
  46.1 0.0 copy-done.12
  46.1 0.2 copy-done.7
  46.3 0.0 copy-start.9
  46.3 0.0 copy-start.6
  46.3 7.6 %outer.1 = (f32[32,64,128]{2,1,0:T(8,128)}, bf16[8,4,16,128]{3,2,1,0:T(8,128)(2,1)}) custom-call(bf16[4,2,32,1152]{3,2,1,0:T(8,128)(2,1)} %bitcast.21, f32[32,64,128]{2,1,0:T(8,128)} %pair_ref.1, bf16[4096,512]{1,0:T(8,128)(2,1)} %weights.1.weight_ref, f32[1,128]{1,0:T(1,128)} %bitcast.30, bf16[8,128]{1,0:T(8,128)(2,1)} %bitcast.26, ...), custom_call_target="tpu_custom_call" | custom-call | flops 2684354560 | bytes 4194304 | tf_op jit(solution)/shard_map/outer/pallas_call | solution.py:496
  53.9 0.0 copy-start
  53.9 0.0 copy-start.1
  53.9 0.0 copy-start.2
  53.9 0.0 copy-start.3
  53.9 4.0 %all-to-all-start.2 = ((bf16[32,16,128]{2,1,0:T(8,128)(2,1)}), bf16[32,16,128]{2,1,0:T(8,128)(2,1)S(1)}, u32[]{:S(2)}, u32[]{:S(2)}) async-start(bf16[32,16,128]{2,1,0:T(8,128)(2,1)} %bitcast.23), calls=%async_computation.2 | async-start | bytes 262144 | tf_op jit(solution)/shard_map/all_to_all | solution.py:533
  57.9 2.7 %collective-permute-start.5 = (bf16[3,32,1024]{2,1,0:T(8,128)(2,1)}, bf16[3,32,1024]{2,1,0:T(8,128)(2,1)S(1)}, u32[]{:S(2)}, u32[]{:S(2)}) collective-permute-start(bf16[3,32,1024]{2,1,0:T(8,128)(2,1)} %get-tuple-element.22), channel_id=1, source_target_pairs={{0,12},{4,8},{8,4},{12,0},{16,28},{20,24},{24,20},{28,16},{1,13},{... | collective-permute-start | bytes 589832 | tf_op jit(solution)/shard_map/ppermute | solution.py:45
  60.7 2.4 %collective-permute-start.6 = (bf16[3,32,1024]{2,1,0:T(8,128)(2,1)}, bf16[3,32,1024]{2,1,0:T(8,128)(2,1)S(1)}, u32[]{:S(2)}, u32[]{:S(2)}) collective-permute-start(bf16[3,32,1024]{2,1,0:T(8,128)(2,1)} %get-tuple-element.23), channel_id=1, source_target_pairs={{0,16},{4,20},{8,24},{12,28},{16,0},{20,4},{24,8},{28,12},{1,17},{... | collective-permute-start | bytes 589832 | tf_op jit(solution)/shard_map/ppermute | solution.py:45
  63.1 0.5 collective-permute-start.7
  63.6 0.0 collective-permute-done.3.refs_1_
  63.6 2.4 %collective-permute-start.8 = (bf16[3,32,1024]{2,1,0:T(8,128)(2,1)}, bf16[3,32,1024]{2,1,0:T(8,128)(2,1)S(1)}, u32[]{:S(2)}, u32[]{:S(2)}) collective-permute-start(bf16[3,32,1024]{2,1,0:T(8,128)(2,1)} %get-tuple-element.25), channel_id=1, source_target_pairs={{0,24},{4,28},{8,16},{12,20},{16,8},{20,12},{24,0},{28,4},{1,25},{... | collective-permute-start | bytes 589832 | tf_op jit(solution)/shard_map/ppermute | solution.py:45
  66.0 0.0 collective-permute-done.4.refs_2_
  66.0 0.0 copy-done.9
  66.0 2.4 %collective-permute-start.9 = (bf16[3,32,1024]{2,1,0:T(8,128)(2,1)S(1)}, bf16[3,32,1024]{2,1,0:T(8,128)(2,1)S(1)}, u32[]{:S(2)}, u32[]{:S(2)}) collective-permute-start(bf16[3,32,1024]{2,1,0:T(8,128)(2,1)S(1)} %copy-done.9), channel_id=1, source_target_pairs={{0,28},{4,24},{8,20},{12,16},{16,12},{20,8},{24,4},{28,0},{1,29},{... | collective-permute-start | bytes 589832 | tf_op jit(solution)/shard_map/ppermute | solution.py:45
  68.3 1.0 mask.1.mask_ref
  69.4 3.2 %collective-permute-done.5.refs_3_ = bf16[3,32,1024]{2,1,0:T(8,128)(2,1)S(1)} collective-permute-done((bf16[3,32,1024]{2,1,0:T(8,128)(2,1)}, bf16[3,32,1024]{2,1,0:T(8,128)(2,1)S(1)}, u32[]{:S(2)}, u32[]{:S(2)}) %collective-permute-start.5) | collective-permute-done | bytes 196640 | tf_op jit(solution)/shard_map/ppermute | solution.py:45
  72.6 13.8 %collective-permute-done.6.refs_4_ = bf16[3,32,1024]{2,1,0:T(8,128)(2,1)S(1)} collective-permute-done((bf16[3,32,1024]{2,1,0:T(8,128)(2,1)}, bf16[3,32,1024]{2,1,0:T(8,128)(2,1)S(1)}, u32[]{:S(2)}, u32[]{:S(2)}) %collective-permute-start.6) | collective-permute-done | bytes 196640 | tf_op jit(solution)/shard_map/ppermute | solution.py:45
  86.4 4.5 %collective-permute-done.7.refs_5_ = bf16[3,32,1024]{2,1,0:T(8,128)(2,1)S(1)} collective-permute-done((bf16[3,32,1024]{2,1,0:T(8,128)(2,1)}, bf16[3,32,1024]{2,1,0:T(8,128)(2,1)S(1)}, u32[]{:S(2)}, u32[]{:S(2)}) %collective-permute-start.7) | collective-permute-done | bytes 196640 | tf_op jit(solution)/shard_map/ppermute | solution.py:45
  90.9 0.0 collective-permute-done.8.refs_6_
  90.9 0.0 collective-permute-done.9.refs_7_
  90.9 0.0 all-to-all-done.2
  90.9 0.0 copy-done.6
  91.0 7.1 %attention.1 = bf16[8,32,1024]{2,1,0:T(8,128)(2,1)} custom-call(bf16[8,4,16,128]{3,2,1,0:T(8,128)(2,1)S(1)} %bitcast.16, f32[8,4,256]{2,1,0:T(4,128)S(1)} %mask.1.mask_ref, bf16[3,32,1024]{2,1,0:T(8,128)(2,1)S(1)} %copy-done.6, bf16[3,32,1024]{2,1,0:T(8,128)(2,1)S(1)} %collective-permute-done.3.refs_1_, ...), custom_call_target="tpu_custom_call" | custom-call | flops 1073741824 | bytes 2097152 | tf_op jit(solution)/shard_map/attention/pallas_call | solution.py:541
  98.0 10.7 %all-to-all-start.3 = ((bf16[8,32,1024]{2,1,0:T(8,128)(2,1)}), bf16[8,32,1024]{2,1,0:T(8,128)(2,1)S(1)}, u32[]{:S(2)}, u32[]{:S(2)}) async-start(bf16[8,32,1024]{2,1,0:T(8,128)(2,1)} %attention.1), calls=%async_computation.3 | async-start | bytes 1048576 | tf_op jit(solution)/shard_map/all_to_all | solution.py:565
  108.7 2.0 %widen.1.wide_ref = bf16[1024,256]{1,0:T(8,128)(2,1)} custom-call(bf16[256,256]{1,0:T(8,128)(2,1)} %out_w_ref.1), custom_call_target="tpu_custom_call" | custom-call | flops 268435456 | bytes 524288 | tf_op jit(solution)/shard_map/widen/pallas_call | solution.py:487
  110.7 11.8 %all-to-all-done.3.mixed_ref = bf16[8,32,1024]{2,1,0:T(8,128)(2,1)S(1)} async-done(((bf16[8,32,1024]{2,1,0:T(8,128)(2,1)}), bf16[8,32,1024]{2,1,0:T(8,128)(2,1)S(1)}, u32[]{:S(2)}, u32[]{:S(2)}) %all-to-all-start.3) | async-done | bytes 524320 | tf_op jit(solution)/shard_map/all_to_all | solution.py:565
  122.5 0.0 copy-done
  122.5 0.0 copy-done.1
  122.5 0.0 copy-done.2
  122.5 0.0 copy-done.3
  122.5 0.0 copy-start.4
  122.6 1.0 copy-done.4
  123.6 0.0 copy-start.5
  123.6 1.2 copy-done.5
  124.8 3.6 %finish.1 = f32[32,32,256]{2,1,0:T(8,128)} custom-call(bf16[8,32,1024]{2,1,0:T(8,128)(2,1)S(1)} %all-to-all-done.3.mixed_ref, f32[8,32,1024]{2,1,0:T(8,128)S(1)} %copy-done.5, bf16[32,32,256]{2,1,0:T(8,128)(2,1)S(1)} %copy-done, bf16[1024,256]{1,0:T(8,128)(2,1)S(1)} %copy-done.4, f32[1,256]{1,0:T(1,128)S(1)} %bitcast.19, bf16[256,1024]{1,0:T(8,128)(2,1)S(1)} %copy-done.1, ...), custom_call_target="tpu_custom_call" | custom-call | flops 1610612736 | bytes 4194304 | tf_op jit(solution)/shard_map/finish/pallas_call | solution.py:579
Async XLA Ops:
  27.9 17.5 %all-to-all-start.1 = ((bf16[8,32,1152]{2,1,0:T(8,128)(2,1)}), bf16[8,32,1152]{2,1,0:T(8,128)(2,1)S(1)}, u32[]{:S(2)}, u32[]{:S(2)}) async-start(bf16[8,32,1152]{2,1,0:T(8,128)(2,1)} %all_to_all.20.rows_ref), calls=%async_computation.1 | async-start | bytes 1179648 | tf_op jit(solution)/shard_map/all_to_all | solution.py:461
  31.4 9.9 %copy-start.8 = (bf16[1024,128]{1,0:T(8,128)(2,1)S(1)}, bf16[1024,128]{1,0:T(8,128)(2,1)}, u32[]{:S(2)}) copy-start(bf16[1024,128]{1,0:T(8,128)(2,1)} %param.26) | copy-start | bytes 786436
  31.4 14.0 %collective-permute-start = (bf16[32,1152]{1,0:T(8,128)(2,1)}, bf16[32,1152]{1,0:T(8,128)(2,1)S(1)}, u32[]{:S(2)}, u32[]{:S(2)}) collective-permute-start(bf16[32,1152]{1,0:T(8,128)(2,1)} %get-tuple-element.16.refs_0_), channel_id=1, source_target_pairs={{0,1},{1,0},{2,3},{3,2},{4,5},{5,4},{6,7},{7,6},{8,9},{9,8},{10,11... | collective-permute-start | bytes 221192 | tf_op jit(solution)/shard_map/ppermute | solution.py:45
  31.9 13.5 %collective-permute-start.1 = (bf16[32,1152]{1,0:T(8,128)(2,1)}, bf16[32,1152]{1,0:T(8,128)(2,1)S(1)}, u32[]{:S(2)}, u32[]{:S(2)}) collective-permute-start(bf16[32,1152]{1,0:T(8,128)(2,1)} %get-tuple-element.16.refs_0_), channel_id=1, source_target_pairs={{0,2},{1,3},{2,0},{3,1},{4,6},{5,7},{6,4},{7,5},{8,10},{9,11},{10,... | collective-permute-start | bytes 221192 | tf_op jit(solution)/shard_map/ppermute | solution.py:45
  33.5 11.9 %collective-permute-start.2 = (bf16[32,1152]{1,0:T(8,128)(2,1)}, bf16[32,1152]{1,0:T(8,128)(2,1)S(1)}, u32[]{:S(2)}, u32[]{:S(2)}) collective-permute-start(bf16[32,1152]{1,0:T(8,128)(2,1)} %get-tuple-element.16.refs_0_), channel_id=1, source_target_pairs={{0,3},{1,2},{2,1},{3,0},{4,7},{5,6},{6,5},{7,4},{8,11},{9,10},{10,... | collective-permute-start | bytes 221192 | tf_op jit(solution)/shard_map/ppermute | solution.py:45
  40.0 23.6 %collective-permute-start.3 = (bf16[3,32,1024]{2,1,0:T(8,128)(2,1)}, bf16[3,32,1024]{2,1,0:T(8,128)(2,1)S(1)}, u32[]{:S(2)}, u32[]{:S(2)}) collective-permute-start(bf16[3,32,1024]{2,1,0:T(8,128)(2,1)} %get-tuple-element.20), channel_id=1, source_target_pairs={{0,4},{4,0},{8,12},{12,8},{16,20},{20,16},{24,28},{28,24},{1,5},{5... | collective-permute-start | bytes 589832 | tf_op jit(solution)/shard_map/ppermute | solution.py:45
  40.9 25.1 %collective-permute-start.4 = (bf16[3,32,1024]{2,1,0:T(8,128)(2,1)}, bf16[3,32,1024]{2,1,0:T(8,128)(2,1)S(1)}, u32[]{:S(2)}, u32[]{:S(2)}) collective-permute-start(bf16[3,32,1024]{2,1,0:T(8,128)(2,1)} %get-tuple-element.21), channel_id=1, source_target_pairs={{0,8},{4,12},{8,0},{12,4},{16,24},{20,28},{24,16},{28,20},{1,9},{5... | collective-permute-start | bytes 589832 | tf_op jit(solution)/shard_map/ppermute | solution.py:45
  45.4 0.6 copy-start.10
  45.4 0.7 copy-start.11
  45.4 0.7 copy-start.12
  45.4 0.9 copy-start.7
  46.3 19.7 %copy-start.9 = (bf16[3,32,1024]{2,1,0:T(8,128)(2,1)S(1)}, bf16[3,32,1024]{2,1,0:T(8,128)(2,1)}, u32[]{:S(2)}) copy-start(bf16[3,32,1024]{2,1,0:T(8,128)(2,1)} %get-tuple-element.26) | copy-start | bytes 589828
  46.3 44.7 %copy-start.6 = (bf16[3,32,1024]{2,1,0:T(8,128)(2,1)S(1)}, bf16[3,32,1024]{2,1,0:T(8,128)(2,1)}, u32[]{:S(2)}) copy-start(bf16[3,32,1024]{2,1,0:T(8,128)(2,1)} %get-tuple-element.19.refs_0_) | copy-start | bytes 589828
  53.9 68.6 %copy-start = (bf16[32,32,256]{2,1,0:T(8,128)(2,1)S(1)}, bf16[32,32,256]{2,1,0:T(8,128)(2,1)}, u32[]{:S(2)}) copy-start(bf16[32,32,256]{2,1,0:T(8,128)(2,1)} %x_ref.1) | copy-start | bytes 1572868
  53.9 68.6 %copy-start.1 = (bf16[256,1024]{1,0:T(8,128)(2,1)S(1)}, bf16[256,1024]{1,0:T(8,128)(2,1)}, u32[]{:S(2)}) copy-start(bf16[256,1024]{1,0:T(8,128)(2,1)} %up_ref.1) | copy-start | bytes 1572868
  53.9 68.6 %copy-start.2 = (bf16[1024,256]{1,0:T(8,128)(2,1)S(1)}, bf16[1024,256]{1,0:T(8,128)(2,1)}, u32[]{:S(2)}) copy-start(bf16[1024,256]{1,0:T(8,128)(2,1)} %down_ref.1) | copy-start | bytes 1572868
  53.9 68.6 %copy-start.3 = (f32[256]{0:T(256)S(1)}, f32[256]{0:T(256)}, u32[]{:S(2)}) copy-start(f32[256]{0:T(256)} %param.35) | copy-start | bytes 3076
  53.9 37.0 %all-to-all-start.2 = ((bf16[32,16,128]{2,1,0:T(8,128)(2,1)}), bf16[32,16,128]{2,1,0:T(8,128)(2,1)S(1)}, u32[]{:S(2)}, u32[]{:S(2)}) async-start(bf16[32,16,128]{2,1,0:T(8,128)(2,1)} %bitcast.23), calls=%async_computation.2 | async-start | bytes 262144 | tf_op jit(solution)/shard_map/all_to_all | solution.py:533
  57.9 14.6 %collective-permute-start.5 = (bf16[3,32,1024]{2,1,0:T(8,128)(2,1)}, bf16[3,32,1024]{2,1,0:T(8,128)(2,1)S(1)}, u32[]{:S(2)}, u32[]{:S(2)}) collective-permute-start(bf16[3,32,1024]{2,1,0:T(8,128)(2,1)} %get-tuple-element.22), channel_id=1, source_target_pairs={{0,12},{4,8},{8,4},{12,0},{16,28},{20,24},{24,20},{28,16},{1,13},{... | collective-permute-start | bytes 589832 | tf_op jit(solution)/shard_map/ppermute | solution.py:45
  60.7 25.7 %collective-permute-start.6 = (bf16[3,32,1024]{2,1,0:T(8,128)(2,1)}, bf16[3,32,1024]{2,1,0:T(8,128)(2,1)S(1)}, u32[]{:S(2)}, u32[]{:S(2)}) collective-permute-start(bf16[3,32,1024]{2,1,0:T(8,128)(2,1)} %get-tuple-element.23), channel_id=1, source_target_pairs={{0,16},{4,20},{8,24},{12,28},{16,0},{20,4},{24,8},{28,12},{1,17},{... | collective-permute-start | bytes 589832 | tf_op jit(solution)/shard_map/ppermute | solution.py:45
  63.1 27.8 %collective-permute-start.7 = (bf16[3,32,1024]{2,1,0:T(8,128)(2,1)}, bf16[3,32,1024]{2,1,0:T(8,128)(2,1)S(1)}, u32[]{:S(2)}, u32[]{:S(2)}) collective-permute-start(bf16[3,32,1024]{2,1,0:T(8,128)(2,1)} %get-tuple-element.24), channel_id=1, source_target_pairs={{0,20},{4,16},{8,28},{12,24},{16,4},{20,0},{24,12},{28,8},{1,21},{... | collective-permute-start | bytes 589832 | tf_op jit(solution)/shard_map/ppermute | solution.py:45
  63.6 27.3 %collective-permute-start.8 = (bf16[3,32,1024]{2,1,0:T(8,128)(2,1)}, bf16[3,32,1024]{2,1,0:T(8,128)(2,1)S(1)}, u32[]{:S(2)}, u32[]{:S(2)}) collective-permute-start(bf16[3,32,1024]{2,1,0:T(8,128)(2,1)} %get-tuple-element.25), channel_id=1, source_target_pairs={{0,24},{4,28},{8,16},{12,20},{16,8},{20,12},{24,0},{28,4},{1,25},{... | collective-permute-start | bytes 589832 | tf_op jit(solution)/shard_map/ppermute | solution.py:45
  66.0 25.0 %collective-permute-start.9 = (bf16[3,32,1024]{2,1,0:T(8,128)(2,1)S(1)}, bf16[3,32,1024]{2,1,0:T(8,128)(2,1)S(1)}, u32[]{:S(2)}, u32[]{:S(2)}) collective-permute-start(bf16[3,32,1024]{2,1,0:T(8,128)(2,1)S(1)} %copy-done.9), channel_id=1, source_target_pairs={{0,28},{4,24},{8,20},{12,16},{16,12},{20,8},{24,4},{28,0},{1,29},{... | collective-permute-start | bytes 589832 | tf_op jit(solution)/shard_map/ppermute | solution.py:45
  98.0 24.5 %all-to-all-start.3 = ((bf16[8,32,1024]{2,1,0:T(8,128)(2,1)}), bf16[8,32,1024]{2,1,0:T(8,128)(2,1)S(1)}, u32[]{:S(2)}, u32[]{:S(2)}) async-start(bf16[8,32,1024]{2,1,0:T(8,128)(2,1)} %attention.1), calls=%async_computation.3 | async-start | bytes 1048576 | tf_op jit(solution)/shard_map/all_to_all | solution.py:565
  122.5 1.0 copy-start.4
  123.6 1.2 copy-start.5

commit v2 on v1

--- a/solution.py
+++ b/solution.py
@@ -38,7 +38,7 @@
 
 def swapped(arrays, axis):
     size = lax.axis_size(axis)
-    assert size & (size - 1) == 0
+    assert len(arrays) & (len(arrays) - 1) == 0 and size % len(arrays) == 0
     come = []
     for k, array in enumerate(arrays):
         pairs = [(i, i ^ k) for i in range(size)]
@@ -97,14 +97,9 @@
     )
     live_plain = dot(live, where_matrix((residues, LANES), lambda r, l: r == l)).astype(BF16)
     lane = lax.broadcasted_iota(jnp.int32, (groups * seqs, span), 1)
-    for wide, out_refs, live_wide, place_of in (
-        (left_wide, [left_ref], live_left, lane // width),
-        (
-            right_wide,
-            [right_ref.at[copy] for copy in range(right_ref.shape[0])],
-            live_right,
-            lane % PACK,
-        ),
+    for wide, out_ref, live_wide, place_of in (
+        (left_wide, left_ref, live_left, lane // width),
+        (right_wide, right_ref, live_right, lane % PACK),
     ):
         product = dot(rows, wide)
         packed = product[: groups * seqs]
@@ -118,15 +113,13 @@
         for group in range(groups):
             piece = packed[group * seqs : (group + 1) * seqs]
             pieces.append((piece * live_wide[:, group * span : (group + 1) * span]).astype(BF16))
-        for out_ref in out_refs:
-            for group in range(groups):
-                out_ref[:, group * span : (group + 1) * span] = pieces[group]
-            out_ref[:, total:] = live_plain
-
-
-def project_kernel(sizes, x_ref, gain_ref, qw_ref, kw_ref, vw_ref, gw_ref, *refs):
-    seqs, residues, heads, head, shares, query_scale = sizes
-    *sent_refs, gate_ref, rows_ref, qkv_ref = refs
+        for group in range(groups):
+            out_ref[:, group * span : (group + 1) * span] = pieces[group]
+        out_ref[:, total:] = live_plain
+
+
+def project_heads(sizes, x_ref, gain_ref, rows_ref, w_refs, write):
+    seqs, residues, heads, head, shares = sizes
     pack = LANES // head
     groups = seqs // pack
     block = groups * residues
@@ -134,45 +127,53 @@
     for seq in range(seqs):
         at = (seq % pack) * block + (seq // pack) * residues
         rows_ref[at : at + residues, :] = norm[seq * residues : (seq + 1) * residues]
-    features = heads * head
     pair = 2 * LANES
-    lane = lax.broadcasted_iota(jnp.int32, (block, pair), 1)
-    place_of = (lane % LANES) // head
+    place_of = (lax.broadcasted_iota(jnp.int32, (block, pair), 1) % LANES) // head
     own = groups // shares
-    for kind, w_ref in enumerate((qw_ref, kw_ref, vw_ref, gw_ref)):
+    for kind, w_ref in enumerate(w_refs):
         for two in range(heads // 2):
             base = two * 2 * head
             spread = where_matrix(
-                (features, pair),
-                lambda r, l: r == base + (l // LANES) * head + l % head,
+                (heads * head, pair), lambda r, l: r == base + (l // LANES) * head + l % head
             )
-            wide = dot(w_ref[...], spread).astype(BF16)
-            product = dot(rows_ref[...], wide)
+            product = dot(rows_ref[...], dot(w_ref[...], spread).astype(BF16))
             packed = product[:block]
             for place in range(1, pack):
                 packed = jnp.where(
                     place_of == place, product[place * block : (place + 1) * block], packed
                 )
-            if kind == 0:
-                packed = packed * query_scale
-            if kind == 3:
-                packed = jax.nn.sigmoid(packed)
-            else:
-                packed = packed.astype(BF16)
             for one in range(2):
+                done = packed[:, one * LANES : (one + 1) * LANES]
                 for group in range(groups):
-                    piece = packed[
-                        group * residues : (group + 1) * residues, one * LANES : (one + 1) * LANES
-                    ]
                     to = (two * 2 + one) * shares + group // own
                     lanes = slice((group % own) * LANES, (group % own + 1) * LANES)
-                    if kind == 3:
-                        gate_ref[to, :, lanes] = piece
-                    else:
-                        qkv_ref[to, kind, :, lanes] = piece
+                    write(kind, to, lanes, done[group * residues : (group + 1) * residues])
+
+
+def gate_kernel(sizes, x_ref, gain_ref, w_ref, gate_ref, rows_ref):
+    def write(kind, to, lanes, piece):
+        gate_ref[to, :, lanes] = jax.nn.sigmoid(piece)
+
+    project_heads(sizes, x_ref, gain_ref, rows_ref, [w_ref], write)
+
+
+def project_kernel(sizes, scale, x_ref, gain_ref, qw_ref, kw_ref, vw_ref, *refs):
+    *sent_refs, rows_ref, qkv_ref = refs
+
+    def write(kind, to, lanes, piece):
+        qkv_ref[to, kind, :, lanes] = (piece * scale if kind == 0 else piece).astype(BF16)
+
+    project_heads(sizes, x_ref, gain_ref, rows_ref, [qw_ref, kw_ref, vw_ref], write)
     me = lax.axis_index("seq")
     for offset, sent_ref in enumerate(sent_refs):
         sent_ref[...] = qkv_ref[me ^ offset]
+
+
+def assemble_kernel(*refs):
+    *part_refs, out_ref = refs
+    me = lax.axis_index("seq")
+    for offset, part_ref in enumerate(part_refs):
+        out_ref[me ^ offset] = part_ref[...]
 
 
 def mask_kernel(sizes, rows_ref, out_ref):
@@ -193,17 +194,6 @@
         out_ref[group] = added[group * pack : (group + 1) * pack]
 
 
-def weight_kernel(sizes, outer_w_ref, blocks_ref):
-    width, pair_width = sizes
-    quad = LANES // width
-    blocks_ref[...] = jnp.zeros_like(blocks_ref)
-    for e in range(width):
-        piece = outer_w_ref[e * width : (e + 1) * width, :]
-        for place in range(quad):
-            row = e * LANES + place * width
-            blocks_ref[row : row + width, place * pair_width : (place + 1) * pair_width] = piece
-
-
 def widen_kernel(sizes, out_w_ref, wide_ref):
     heads, head = sizes
     spread = where_matrix(
@@ -217,18 +207,23 @@
     members = right_ref.shape[0]
     left_refs = refs[:members]
     out_ref, bias_ref, left_ref, stage_ref, norm_ref, bias_rows_ref = refs[members : members + 6]
-    held_ref, held_pair_ref, weight_sem, pair_sem = refs[members + 6 :]
-    weight_copy = pltpu.make_async_copy(weight_ref, held_ref, weight_sem)
-    weight_copy.start()
+    held_ref, plain_ref, held_pair_ref, pair_sem = refs[members + 6 :]
     pair_copy = pltpu.make_async_copy(pair_ref, held_pair_ref, pair_sem)
     pair_copy.start()
+    quad = LANES // width
+    plain_ref[...] = weight_ref[...].astype(F32)
+    held_ref[...] = jnp.zeros_like(held_ref)
+    for e in range(width):
+        piece = plain_ref[pl.ds(e, width, stride=width), :].astype(BF16)
+        for place in range(quad):
+            row = e * LANES + place * width
+            held_ref[row : row + width, place * pair_width : (place + 1) * pair_width] = piece
     share = seqs // members
     me = lax.axis_index("res")
     for offset, member_ref in enumerate(left_refs):
         at = pl.multiple_of((me ^ offset) * share, share)
         left_ref[pl.ds(at, share), :] = member_ref[...]
     span = PACK * width
-    quad = LANES // width
     groups = residues // quad
     total = residues * width
     blocks = right_ref.shape[1]
@@ -257,7 +252,6 @@
                         ]
     scale = 1.0 / jnp.maximum(jnp.concatenate(counts, axis=0), 1.0)
     gain = gain_ref[...]
-    weight_copy.wait()
     pair_copy.wait()
     for two in range(quad // 2):
         lanes = slice(two * 2 * pair_width, (two + 1) * 2 * pair_width)
@@ -418,10 +412,7 @@
 
     left, right = pl.pallas_call(
         functools.partial(factor_kernel, (seqs, residues, width)),
-        out_shape=(
-            jax.ShapeDtypeStruct((seqs, wide), BF16),
-            jax.ShapeDtypeStruct((seq_axis, seqs, wide), BF16),
-        ),
+        out_shape=(jax.ShapeDtypeStruct((seqs, wide), BF16),) * 2,
         scratch_shapes=[
             pltpu.VMEM((channels // LANES, seqs * residues, LANES), F32),
             pltpu.VMEM((seqs * residues, channels), BF16),
@@ -434,29 +425,47 @@
         name="factors",
     )(flat, alignment_mask, residue_mask[None], outer_gain[None], left_weight.T, right_weight.T)
 
-    right_rows = lax.all_to_all(right, "seq", split_axis=0, concat_axis=0, tiled=True)
+    half = seq_axis // 2
+    come = lax.ppermute(right, "seq", [(i, i ^ half) for i in range(seq_axis)])
+    right_parts = swapped([right] * half, "seq")
+    right_parts = right_parts + swapped([come] * half, "seq")
+
     left_all = swapped([left] * res_axis, "res")
 
-    *qkv, gates = pl.pallas_call(
-        functools.partial(
-            project_kernel,
-            (seqs, residues, heads, head, shares, head ** (-0.5) * math.log2(math.e)),
-        ),
-        out_shape=(
-            *(jax.ShapeDtypeStruct((3, residues, own * head), BF16),) * seq_axis,
-            jax.ShapeDtypeStruct((seq_axis, residues, own * head), F32),
-        ),
+    head_sizes = (seqs, residues, heads, head, shares)
+    qkv = pl.pallas_call(
+        functools.partial(project_kernel, head_sizes, head ** (-0.5) * math.log2(math.e)),
+        out_shape=(jax.ShapeDtypeStruct((3, residues, own * head), BF16),) * seq_axis,
         scratch_shapes=[
             pltpu.VMEM((seqs * residues, channels), BF16),
             pltpu.VMEM((seq_axis, 3, residues, own * head), BF16),
         ],
         compiler_params=params(ALL_VMEM_BYTES),
         cost_estimate=pl.CostEstimate(
-            flops=2 * seqs * residues * channels * 4 * heads * LANES, bytes_accessed=4 << 20,
+            flops=2 * seqs * residues * channels * 3 * heads * LANES, bytes_accessed=2 << 20,
+            transcendentals=0,
+        ),
+        name="projections",
+    )(flat, row_gain[None], query_weight, key_weight, value_weight)
+    gates = pl.pallas_call(
+        functools.partial(gate_kernel, head_sizes),
+        out_shape=jax.ShapeDtypeStruct((seq_axis, residues, own * head), F32),
+        scratch_shapes=[pltpu.VMEM((seqs * residues, channels), BF16)],
+        compiler_params=params(ALL_VMEM_BYTES),
+        cost_estimate=pl.CostEstimate(
+            flops=2 * seqs * residues * channels * heads * LANES, bytes_accessed=2 << 20,
             transcendentals=seqs * residues * channels,
         ),
-        name="projections",
-    )(flat, row_gain[None], query_weight, key_weight, value_weight, gate_weight)
+        name="gates",
+    )(flat, row_gain[None], gate_weight)
+
+    right_rows = pl.pallas_call(
+        assemble_kernel,
+        out_shape=jax.ShapeDtypeStruct((seq_axis, seqs, wide), BF16),
+        compiler_params=params(),
+        cost_estimate=pl.CostEstimate(flops=1 << 26, bytes_accessed=1 << 20, transcendentals=0),
+        name="assemble",
+    )(*right_parts)
 
     right_all = lax.all_to_all(right_rows, "res", split_axis=0, concat_axis=0, tiled=True)
     qkv_all = swapped(qkv, "seq")
@@ -474,16 +483,7 @@
         name="mask",
     )(right_rows)
 
-    flipped_w = outer_weight.reshape(width, width, pair_width).swapaxes(0, 1)
-    flipped_w = flipped_w.reshape(width * width, pair_width)
     quad = LANES // width
-    wide_outer = pl.pallas_call(
-        functools.partial(weight_kernel, (width, pair_width)),
-        out_shape=jax.ShapeDtypeStruct((width * LANES, quad * pair_width), BF16),
-        compiler_params=params(ALL_VMEM_BYTES),
-        cost_estimate=pl.CostEstimate(flops=1 << 29, bytes_accessed=5 << 20, transcendentals=0),
-        name="weights",
-    )(flipped_w)
     wide_output = pl.pallas_call(
         functools.partial(widen_kernel, (heads, head)),
         out_shape=jax.ShapeDtypeStruct((heads * LANES, channels), BF16),
@@ -498,7 +498,7 @@
             outer_kernel, (residues, columns, width, pair_width, all_seqs, shares)
         ),
         in_specs=[
-            pl.BlockSpec(memory_space=pl.ANY if at in (1, 2) else pltpu.VMEM)
+            pl.BlockSpec(memory_space=pl.ANY if at == 1 else pltpu.VMEM)
             for at in range(5 + res_axis)
         ],
         out_shape=(
@@ -511,8 +511,8 @@
             pltpu.VMEM((residues, columns, pair_width), BF16),
             pltpu.VMEM((heads, bias_rows, LANES), F32),
             pltpu.VMEM((width * LANES, quad * pair_width), BF16),
+            pltpu.VMEM(outer_weight.shape, F32),
             pltpu.VMEM(pair_input.shape, F32),
-            pltpu.SemaphoreType.DMA,
             pltpu.SemaphoreType.DMA,
         ],
         compiler_params=params(ALL_VMEM_BYTES),
@@ -525,7 +525,7 @@
     )(
         right_all.reshape(res_axis, blocks, seqs, wide),
         pair_input,
-        wide_outer,
+        outer_weight,
         pair_gain[None],
         bias_weight.T,
         *left_all,

time: 129 us -> 120 us (0.930)
  blocking collectives: 23.9 us -> 0 us
  starting transfers between devices: 31.8 us -> 44.1 us
  waiting for transfers between devices: 33.4 us -> 36.7 us
    all_to_all x1 -> x0, blocking collectives: 23.9 us -> none  [on_device(): lax.all_to_all(right, 'seq', split_axis=0, concat_axis=0, tiled=True)]
    ppermute x10 -> x16, starting transfers between devices: 13.7 us -> 21.9 us  [swapped(): come.append(lax.ppermute(array, axis, pairs) if k else array)]
    ppermute x10 -> x16, waiting for transfers between devices: 21.6 us -> 27.9 us  [swapped(): come.append(lax.ppermute(array, axis, pairs) if k else array)]
    ppermute x0 -> x1, starting transfers between devices: none -> 4.06 us  [on_device(): come = lax.ppermute(right, 'seq', [(i, i ^ half) for i in range(seq_axis)])]
    all_to_all x1, waiting for transfers between devices: 11.8 us -> 8.49 us  [on_device(): lax.all_to_all(mixed, 'seq', split_axis=0, concat_axis=0, tiled=True)]
    unnamed x26 -> x36, local copies, waits for them, and re-layouts: 3.15 us -> 4.02 us
    pallas_call x2 -> x3, Pallas kernels: 9.87 us -> 10.1 us  [the longest x1 5.68 us: on_device(): pl.pallas_call(functools.partial(project_kernel, head_sizes, head ** (-0....]
  transfers between devices with their start and end apart: 13 -> 20, of which waited for: 4 -> 11; matrix products, arithmetic and copies ran while one was open for 1% -> 0% of each run, Pallas kernels for 16% -> 16%
where the time goes in v2:
time: 120 us
  starting transfers between devices  44.1 us (37%)
  waiting for transfers between devices  36.7 us (31%)
  Pallas kernels  34.2 us (29%)
  local copies, waits for them, and re-layouts  4.02 us (3%)
    ppermute x16, waiting for transfers between devices, swapped(): come.append(lax.ppermute(array, axis, pairs) if k else array)  27.9 us
    ppermute x16, starting transfers between devices, swapped(): come.append(lax.ppermute(array, axis, pairs) if k else array)  21.9 us
    all_to_all x1, starting transfers between devices, on_device(): lax.all_to_all(mixed, 'seq', split_axis=0, concat_axis=0, tiled=True)  10.4 us
    all_to_all x1, waiting for transfers between devices, on_device(): lax.all_to_all(mixed, 'seq', split_axis=0, concat_axis=0, tiled=True)  8.49 us
    pallas_call x1, Pallas kernels, on_device(): pl.pallas_call(functools.partial(outer_kernel, (residues, columns, width,...  7.16 us
    pallas_call x1, Pallas kernels, on_device(): pl.pallas_call(functools.partial(attention_kernel, (residues, columns, he...  7.07 us
    pallas_call x1, Pallas kernels, on_device(): pl.pallas_call(functools.partial(project_kernel, head_sizes, head ** (-0....  5.68 us
    all_to_all x1, starting transfers between devices, on_device(): lax.all_to_all(bias.reshape(seq_axis * res_axis, bias_rows, LANES), ('seq...  4.08 us
  transfers between devices with their start and end apart: 20, of which 11 were waited for; matrix products, arithmetic and copies ran while one was open for 0% of the time, Pallas kernels for 16%

profile of v2, /device:TPU:0, one launch (start us, length us, event | category | flops | bytes accessed | tf_op | source)
XLA Modules:
  0.0 119.8 jit_solution(7555808193369794932)
XLA Ops:
  0.6 3.2 %factors.1 = (bf16[32,1152]{1,0:T(8,128)(2,1)}, bf16[32,1152]{1,0:T(8,128)(2,1)}) custom-call(bf16[1024,256]{1,0:T(8,128)(2,1)} %bitcast.13, s32[32,32]{1,0:T(8,128)} %mask_ref.1, s32[1,256]{1,0:T(1,128)} %bitcast.22, f32[1,256]{1,0:T(1,128)} %bitcast.23, bf16[32,256]{1,0:T(8,128)(2,1)} %bitcast.19, bf16[32,256]{1,0:T(8,128)(2,1)} %bitcast.20), custom_call_target="tpu_custom_call" | custom-call | flops 268435456 | bytes 1048576 | tf_op jit(solution)/shard_map/factors/pallas_call | solution.py:413
  3.8 4.1 %collective-permute-start.3 = (bf16[32,1152]{1,0:T(8,128)(2,1)}, bf16[32,1152]{1,0:T(8,128)(2,1)S(1)}, u32[]{:S(2)}, u32[]{:S(2)}) collective-permute-start(bf16[32,1152]{1,0:T(8,128)(2,1)} %get-tuple-element.14.refs_0_), channel_id=1, source_target_pairs={{0,16},{4,20},{8,24},{12,28},{16,0},{20,4},{24,8},{28,12},{1,17},{... | collective-permute-start | bytes 221192 | tf_op jit(solution)/shard_map/ppermute | solution.py:429
  7.9 1.5 %collective-permute-start = (bf16[32,1152]{1,0:T(8,128)(2,1)}, bf16[32,1152]{1,0:T(8,128)(2,1)S(1)}, u32[]{:S(2)}, u32[]{:S(2)}) collective-permute-start(bf16[32,1152]{1,0:T(8,128)(2,1)} %get-tuple-element.14.refs_0_), channel_id=1, source_target_pairs={{0,4},{4,0},{8,12},{12,8},{16,20},{20,16},{24,28},{28,24},{1,5},{5... | collective-permute-start | bytes 221192 | tf_op jit(solution)/shard_map/ppermute | solution.py:45
  9.4 1.6 %collective-permute-start.1 = (bf16[32,1152]{1,0:T(8,128)(2,1)}, bf16[32,1152]{1,0:T(8,128)(2,1)S(1)}, u32[]{:S(2)}, u32[]{:S(2)}) collective-permute-start(bf16[32,1152]{1,0:T(8,128)(2,1)} %get-tuple-element.14.refs_0_), channel_id=1, source_target_pairs={{0,8},{4,12},{8,0},{12,4},{16,24},{20,28},{24,16},{28,20},{1,9},{5... | collective-permute-start | bytes 221192 | tf_op jit(solution)/shard_map/ppermute | solution.py:45
  10.9 0.4 collective-permute-start.2
  11.4 0.3 collective-permute-done.3.refs_4_
  11.7 1.7 %collective-permute-start.4 = (bf16[32,1152]{1,0:T(8,128)(2,1)S(1)}, bf16[32,1152]{1,0:T(8,128)(2,1)S(1)}, u32[]{:S(2)}, u32[]{:S(2)}) collective-permute-start(bf16[32,1152]{1,0:T(8,128)(2,1)S(1)} %collective-permute-done.3.refs_4_), channel_id=1, source_target_pairs={{0,4},{4,0},{8,12},{12,8},{16,20},{20,16},{24,28},{28,24},{1,5},{5... | collective-permute-start | bytes 221192 | tf_op jit(solution)/shard_map/ppermute | solution.py:45
  13.4 1.1 collective-permute-start.5
  14.4 0.0 collective-permute-done.refs_1_
  14.4 1.3 %collective-permute-start.6 = (bf16[32,1152]{1,0:T(8,128)(2,1)S(1)}, bf16[32,1152]{1,0:T(8,128)(2,1)S(1)}, u32[]{:S(2)}, u32[]{:S(2)}) collective-permute-start(bf16[32,1152]{1,0:T(8,128)(2,1)S(1)} %collective-permute-done.3.refs_4_), channel_id=1, source_target_pairs={{0,12},{4,8},{8,4},{12,0},{16,28},{20,24},{24,20},{28,16},{1,13},{... | collective-permute-start | bytes 221192 | tf_op jit(solution)/shard_map/ppermute | solution.py:45
  15.7 0.0 collective-permute-done.1.refs_2_
  15.7 0.8 collective-permute-done.2.refs_3_
  16.5 0.3 collective-permute-done.4.refs_5_
  16.8 0.9 collective-permute-done.5.refs_6_
  17.7 2.0 %collective-permute-done.6.refs_7_ = bf16[32,1152]{1,0:T(8,128)(2,1)S(1)} collective-permute-done((bf16[32,1152]{1,0:T(8,128)(2,1)S(1)}, bf16[32,1152]{1,0:T(8,128)(2,1)S(1)}, u32[]{:S(2)}, u32[]{:S(2)}) %collective-permute-start.6) | collective-permute-done | bytes 73760 | tf_op jit(solution)/shard_map/ppermute | solution.py:45
  19.7 0.9 copy-done
  20.6 0.9 assemble.1.rows_ref
  21.5 3.6 %all-to-all-start = ((bf16[8,32,1152]{2,1,0:T(8,128)(2,1)}), bf16[8,32,1152]{2,1,0:T(8,128)(2,1)S(1)}, u32[]{:S(2)}, u32[]{:S(2)}) async-start(bf16[8,32,1152]{2,1,0:T(8,128)(2,1)} %assemble.1.rows_ref), calls=%async_computation | async-start | bytes 1179648 | tf_op jit(solution)/shard_map/all_to_all | solution.py:470
  25.1 0.0 copy-done.14
  25.1 0.5 collective-permute-start.7
  25.5 1.6 %collective-permute-start.8 = (bf16[32,1152]{1,0:T(8,128)(2,1)S(1)}, bf16[32,1152]{1,0:T(8,128)(2,1)S(1)}, u32[]{:S(2)}, u32[]{:S(2)}) collective-permute-start(bf16[32,1152]{1,0:T(8,128)(2,1)S(1)} %copy-done.14), channel_id=1, source_target_pairs={{0,2},{1,3},{2,0},{3,1},{4,6},{5,7},{6,4},{7,5},{8,10},{9,11},{10,... | collective-permute-start | bytes 221192 | tf_op jit(solution)/shard_map/ppermute | solution.py:45
  27.2 0.0 collective-permute-start.9
  27.2 5.7 %projections.1 = (bf16[3,32,1024]{2,1,0:T(8,128)(2,1)}, bf16[3,32,1024]{2,1,0:T(8,128)(2,1)}, bf16[3,32,1024]{2,1,0:T(8,128)(2,1)}, bf16[3,32,1024]{2,1,0:T(8,12...) custom-call(bf16[1024,256]{1,0:T(8,128)(2,1)} %bitcast.14, ...), custom_call_target="tpu_custom_call" | custom-call | flops 1610612736 | bytes 2097152 | tf_op jit(solution)/shard_map/projections/pallas_call | solution.py:436
  32.9 0.5 collective-permute-start.10
  33.4 1.3 %collective-permute-start.11 = (bf16[3,32,1024]{2,1,0:T(8,128)(2,1)}, bf16[3,32,1024]{2,1,0:T(8,128)(2,1)S(1)}, u32[]{:S(2)}, u32[]{:S(2)}) collective-permute-start(bf16[3,32,1024]{2,1,0:T(8,128)(2,1)} %get-tuple-element.20), channel_id=1, source_target_pairs={{0,8},{4,12},{8,0},{12,4},{16,24},{20,28},{24,16},{28,20},{1,9},{5... | collective-permute-start | bytes 589832 | tf_op jit(solution)/shard_map/ppermute | solution.py:45
  34.7 0.0 collective-permute-done.7.refs_1_
  34.7 2.0 %collective-permute-done.8.refs_2_ = bf16[32,1152]{1,0:T(8,128)(2,1)S(1)} collective-permute-done((bf16[32,1152]{1,0:T(8,128)(2,1)S(1)}, bf16[32,1152]{1,0:T(8,128)(2,1)S(1)}, u32[]{:S(2)}, u32[]{:S(2)}) %collective-permute-start.8) | collective-permute-done | bytes 73760 | tf_op jit(solution)/shard_map/ppermute | solution.py:45
  36.7 0.4 collective-permute-done.9.refs_3_
  37.1 0.0 all-to-all-done
  37.1 0.0 copy-done.15
  37.1 0.2 copy-done.16
  37.3 0.4 copy-done.17
  37.8 0.2 copy-done.8
  38.0 7.2 %outer.1 = (f32[32,64,128]{2,1,0:T(8,128)}, bf16[8,4,16,128]{3,2,1,0:T(8,128)(2,1)}) custom-call(bf16[4,2,32,1152]{3,2,1,0:T(8,128)(2,1)} %bitcast.17, f32[32,64,128]{2,1,0:T(8,128)} %pair_ref.1, bf16[1024,128]{1,0:T(8,128)(2,1)} %weight_ref.1, f32[1,128]{1,0:T(1,128)} %bitcast.26, bf16[8,128]{1,0:T(8,128)(2,1)} %bitcast.21, ...), custom_call_target="tpu_custom_call" | custom-call | flops 2684354560 | bytes 4194304 | tf_op jit(solution)/shard_map/outer/pallas_call | solution.py:496
  45.2 0.0 copy-start.9
  45.2 4.1 %all-to-all-start.1 = ((bf16[32,16,128]{2,1,0:T(8,128)(2,1)}), bf16[32,16,128]{2,1,0:T(8,128)(2,1)S(1)}, u32[]{:S(2)}, u32[]{:S(2)}) async-start(bf16[32,16,128]{2,1,0:T(8,128)(2,1)} %bitcast.18), calls=%async_computation.1 | async-start | bytes 262144 | tf_op jit(solution)/shard_map/all_to_all | solution.py:533
  49.3 0.0 copy-done.13
  49.3 2.7 %collective-permute-start.12 = (bf16[3,32,1024]{2,1,0:T(8,128)(2,1)S(1)}, bf16[3,32,1024]{2,1,0:T(8,128)(2,1)S(1)}, u32[]{:S(2)}, u32[]{:S(2)}) collective-permute-start(bf16[3,32,1024]{2,1,0:T(8,128)(2,1)S(1)} %copy-done.13), channel_id=1, source_target_pairs={{0,12},{4,8},{8,4},{12,0},{16,28},{20,24},{24,20},{28,16},{1,13},{... | collective-permute-start | bytes 589832 | tf_op jit(solution)/shard_map/ppermute | solution.py:45
  52.0 0.0 copy-done.12
  52.0 2.4 %collective-permute-start.13 = (bf16[3,32,1024]{2,1,0:T(8,128)(2,1)S(1)}, bf16[3,32,1024]{2,1,0:T(8,128)(2,1)S(1)}, u32[]{:S(2)}, u32[]{:S(2)}) collective-permute-start(bf16[3,32,1024]{2,1,0:T(8,128)(2,1)S(1)} %copy-done.12), channel_id=1, source_target_pairs={{0,16},{4,20},{8,24},{12,28},{16,0},{20,4},{24,8},{28,12},{1,17},{... | collective-permute-start | bytes 589832 | tf_op jit(solution)/shard_map/ppermute | solution.py:45
  54.4 0.0 copy-done.11
  54.4 0.5 collective-permute-start.14
  54.9 0.0 collective-permute-done.10.refs_1_
  54.9 0.0 copy-done.10
  54.9 2.4 %collective-permute-start.15 = (bf16[3,32,1024]{2,1,0:T(8,128)(2,1)S(1)}, bf16[3,32,1024]{2,1,0:T(8,128)(2,1)S(1)}, u32[]{:S(2)}, u32[]{:S(2)}) collective-permute-start(bf16[3,32,1024]{2,1,0:T(8,128)(2,1)S(1)} %copy-done.10), channel_id=1, source_target_pairs={{0,24},{4,28},{8,16},{12,20},{16,8},{20,12},{24,0},{28,4},{1,25},{... | collective-permute-start | bytes 589832 | tf_op jit(solution)/shard_map/ppermute | solution.py:45
  57.3 0.0 collective-permute-done.11.refs_2_
  57.3 2.4 %collective-permute-start.16 = (bf16[3,32,1024]{2,1,0:T(8,128)(2,1)S(1)}, bf16[3,32,1024]{2,1,0:T(8,128)(2,1)S(1)}, u32[]{:S(2)}, u32[]{:S(2)}) collective-permute-start(bf16[3,32,1024]{2,1,0:T(8,128)(2,1)S(1)} %copy-done.9), channel_id=1, source_target_pairs={{0,28},{4,24},{8,20},{12,16},{16,12},{20,8},{24,4},{28,0},{1,29},{... | collective-permute-start | bytes 589832 | tf_op jit(solution)/shard_map/ppermute | solution.py:45
  59.7 1.0 mask.1.mask_ref
  60.8 3.1 %collective-permute-done.12.refs_3_ = bf16[3,32,1024]{2,1,0:T(8,128)(2,1)S(1)} collective-permute-done((bf16[3,32,1024]{2,1,0:T(8,128)(2,1)S(1)}, bf16[3,32,1024]{2,1,0:T(8,128)(2,1)S(1)}, u32[]{:S(2)}, u32[]{:S(2)}) %collective-permute-start.12) | collective-permute-done | bytes 196640 | tf_op jit(solution)/shard_map/ppermute | solution.py:45
  63.9 13.7 %collective-permute-done.13.refs_4_ = bf16[3,32,1024]{2,1,0:T(8,128)(2,1)S(1)} collective-permute-done((bf16[3,32,1024]{2,1,0:T(8,128)(2,1)S(1)}, bf16[3,32,1024]{2,1,0:T(8,128)(2,1)S(1)}, u32[]{:S(2)}, u32[]{:S(2)}) %collective-permute-start.13) | collective-permute-done | bytes 196640 | tf_op jit(solution)/shard_map/ppermute | solution.py:45
  77.6 4.6 %collective-permute-done.14.refs_5_ = bf16[3,32,1024]{2,1,0:T(8,128)(2,1)S(1)} collective-permute-done((bf16[3,32,1024]{2,1,0:T(8,128)(2,1)S(1)}, bf16[3,32,1024]{2,1,0:T(8,128)(2,1)S(1)}, u32[]{:S(2)}, u32[]{:S(2)}) %collective-permute-start.14) | collective-permute-done | bytes 196640 | tf_op jit(solution)/shard_map/ppermute | solution.py:45
  82.3 0.0 collective-permute-done.15.refs_6_
  82.3 0.0 collective-permute-done.16.refs_7_
  82.3 0.0 all-to-all-done.1
  82.3 7.1 %attention.1 = bf16[8,32,1024]{2,1,0:T(8,128)(2,1)} custom-call(bf16[8,4,16,128]{3,2,1,0:T(8,128)(2,1)S(1)} %bitcast.12, f32[8,4,256]{2,1,0:T(4,128)S(1)} %mask.1.mask_ref, bf16[3,32,1024]{2,1,0:T(8,128)(2,1)S(1)} %copy-done.7, bf16[3,32,1024]{2,1,0:T(8,128)(2,1)S(1)} %collective-permute-done.10.refs_1_, ...), custom_call_target="tpu_custom_call" | custom-call | flops 1073741824 | bytes 2097152 | tf_op jit(solution)/shard_map/attention/pallas_call | solution.py:541
  89.3 10.4 %all-to-all-start.2 = ((bf16[8,32,1024]{2,1,0:T(8,128)(2,1)}), bf16[8,32,1024]{2,1,0:T(8,128)(2,1)S(1)}, u32[]{:S(2)}, u32[]{:S(2)}) async-start(bf16[8,32,1024]{2,1,0:T(8,128)(2,1)} %attention.1), calls=%async_computation.2 | async-start | bytes 1048576 | tf_op jit(solution)/shard_map/all_to_all | solution.py:565
  99.8 2.0 %widen.1.wide_ref = bf16[1024,256]{1,0:T(8,128)(2,1)} custom-call(bf16[256,256]{1,0:T(8,128)(2,1)} %out_w_ref.1), custom_call_target="tpu_custom_call" | custom-call | flops 268435456 | bytes 524288 | tf_op jit(solution)/shard_map/widen/pallas_call | solution.py:487
  101.8 3.5 %gates.1.gate_ref = f32[8,32,1024]{2,1,0:T(8,128)} custom-call(bf16[1024,256]{1,0:T(8,128)(2,1)} %bitcast.15, f32[1,256]{1,0:T(1,128)} %bitcast.25, bf16[256,256]{1,0:T(8,128)(2,1)} %w_ref.1), custom_call_target="tpu_custom_call" | custom-call | flops 536870912 | bytes 2097152 | tf_op jit(solution)/shard_map/gates/pallas_call | solution.py:450
  105.3 8.5 %all-to-all-done.2.mixed_ref = bf16[8,32,1024]{2,1,0:T(8,128)(2,1)S(1)} async-done(((bf16[8,32,1024]{2,1,0:T(8,128)(2,1)}), bf16[8,32,1024]{2,1,0:T(8,128)(2,1)S(1)}, u32[]{:S(2)}, u32[]{:S(2)}) %all-to-all-start.2) | async-done | bytes 524320 | tf_op jit(solution)/shard_map/all_to_all | solution.py:565
  113.9 0.0 copy-done.4
  113.9 0.0 copy-start.5
  113.9 1.2 %copy-done.5 = f32[8,32,1024]{2,1,0:T(8,128)S(1)} copy-done((f32[8,32,1024]{2,1,0:T(8,128)S(1)}, f32[8,32,1024]{2,1,0:T(8,128)}, u32[]{:S(2)}) %copy-start.5) | copy-done | bytes 1048600
  115.1 1.0 copy-done.6
  116.1 3.6 %finish.1 = f32[32,32,256]{2,1,0:T(8,128)} custom-call(bf16[8,32,1024]{2,1,0:T(8,128)(2,1)S(1)} %all-to-all-done.2.mixed_ref, f32[8,32,1024]{2,1,0:T(8,128)S(1)} %copy-done.5, bf16[32,32,256]{2,1,0:T(8,128)(2,1)S(1)} %copy-done.1, bf16[1024,256]{1,0:T(8,128)(2,1)S(1)} %copy-done.6, f32[1,256]{1,0:T(1,128)S(1)} %bitcast.16, bf16[256,1024]{1,0:T(8,128)(2,1)S(1)} %copy-done.2, ...), custom_call_target="tpu_custom_call" | custom-call | flops 1610612736 | bytes 4194304 | tf_op jit(solution)/shard_map/finish/pallas_call | solution.py:579
  (21 shorter events, 0.0 us)
Async XLA Ops:
  3.8 7.9 %collective-permute-start.3 = (bf16[32,1152]{1,0:T(8,128)(2,1)}, bf16[32,1152]{1,0:T(8,128)(2,1)S(1)}, u32[]{:S(2)}, u32[]{:S(2)}) collective-permute-start(bf16[32,1152]{1,0:T(8,128)(2,1)} %get-tuple-element.14.refs_0_), channel_id=1, source_target_pairs={{0,16},{4,20},{8,24},{12,28},{16,0},{20,4},{24,8},{28,12},{1,17},{... | collective-permute-start | bytes 221192 | tf_op jit(solution)/shard_map/ppermute | solution.py:429
  7.9 6.6 %collective-permute-start = (bf16[32,1152]{1,0:T(8,128)(2,1)}, bf16[32,1152]{1,0:T(8,128)(2,1)S(1)}, u32[]{:S(2)}, u32[]{:S(2)}) collective-permute-start(bf16[32,1152]{1,0:T(8,128)(2,1)} %get-tuple-element.14.refs_0_), channel_id=1, source_target_pairs={{0,4},{4,0},{8,12},{12,8},{16,20},{20,16},{24,28},{28,24},{1,5},{5... | collective-permute-start | bytes 221192 | tf_op jit(solution)/shard_map/ppermute | solution.py:45
  9.4 6.4 %collective-permute-start.1 = (bf16[32,1152]{1,0:T(8,128)(2,1)}, bf16[32,1152]{1,0:T(8,128)(2,1)S(1)}, u32[]{:S(2)}, u32[]{:S(2)}) collective-permute-start(bf16[32,1152]{1,0:T(8,128)(2,1)} %get-tuple-element.14.refs_0_), channel_id=1, source_target_pairs={{0,8},{4,12},{8,0},{12,4},{16,24},{20,28},{24,16},{28,20},{1,9},{5... | collective-permute-start | bytes 221192 | tf_op jit(solution)/shard_map/ppermute | solution.py:45
  10.9 5.6 %collective-permute-start.2 = (bf16[32,1152]{1,0:T(8,128)(2,1)}, bf16[32,1152]{1,0:T(8,128)(2,1)S(1)}, u32[]{:S(2)}, u32[]{:S(2)}) collective-permute-start(bf16[32,1152]{1,0:T(8,128)(2,1)} %get-tuple-element.14.refs_0_), channel_id=1, source_target_pairs={{0,12},{4,8},{8,4},{12,0},{16,28},{20,24},{24,20},{28,16},{1,13},{... | collective-permute-start | bytes 221192 | tf_op jit(solution)/shard_map/ppermute | solution.py:45
  11.7 5.1 %collective-permute-start.4 = (bf16[32,1152]{1,0:T(8,128)(2,1)S(1)}, bf16[32,1152]{1,0:T(8,128)(2,1)S(1)}, u32[]{:S(2)}, u32[]{:S(2)}) collective-permute-start(bf16[32,1152]{1,0:T(8,128)(2,1)S(1)} %collective-permute-done.3.refs_4_), channel_id=1, source_target_pairs={{0,4},{4,0},{8,12},{12,8},{16,20},{20,16},{24,28},{28,24},{1,5},{5... | collective-permute-start | bytes 221192 | tf_op jit(solution)/shard_map/ppermute | solution.py:45
  13.4 4.4 %collective-permute-start.5 = (bf16[32,1152]{1,0:T(8,128)(2,1)S(1)}, bf16[32,1152]{1,0:T(8,128)(2,1)S(1)}, u32[]{:S(2)}, u32[]{:S(2)}) collective-permute-start(bf16[32,1152]{1,0:T(8,128)(2,1)S(1)} %collective-permute-done.3.refs_4_), channel_id=1, source_target_pairs={{0,8},{4,12},{8,0},{12,4},{16,24},{20,28},{24,16},{28,20},{1,9},{5... | collective-permute-start | bytes 221192 | tf_op jit(solution)/shard_map/ppermute | solution.py:45
  14.4 5.3 %collective-permute-start.6 = (bf16[32,1152]{1,0:T(8,128)(2,1)S(1)}, bf16[32,1152]{1,0:T(8,128)(2,1)S(1)}, u32[]{:S(2)}, u32[]{:S(2)}) collective-permute-start(bf16[32,1152]{1,0:T(8,128)(2,1)S(1)} %collective-permute-done.3.refs_4_), channel_id=1, source_target_pairs={{0,12},{4,8},{8,4},{12,0},{16,28},{20,24},{24,20},{28,16},{1,13},{... | collective-permute-start | bytes 221192 | tf_op jit(solution)/shard_map/ppermute | solution.py:45
  19.7 0.9 copy-start
  21.5 3.6 %copy-start.14 = (bf16[32,1152]{1,0:T(8,128)(2,1)S(1)}, bf16[32,1152]{1,0:T(8,128)(2,1)}, u32[]{:S(2)}) copy-start(bf16[32,1152]{1,0:T(8,128)(2,1)} %get-tuple-element.15.refs_0_) | copy-start | bytes 221188
  21.5 15.7 %all-to-all-start = ((bf16[8,32,1152]{2,1,0:T(8,128)(2,1)}), bf16[8,32,1152]{2,1,0:T(8,128)(2,1)S(1)}, u32[]{:S(2)}, u32[]{:S(2)}) async-start(bf16[8,32,1152]{2,1,0:T(8,128)(2,1)} %assemble.1.rows_ref), calls=%async_computation | async-start | bytes 1179648 | tf_op jit(solution)/shard_map/all_to_all | solution.py:470
  25.1 9.6 %collective-permute-start.7 = (bf16[32,1152]{1,0:T(8,128)(2,1)S(1)}, bf16[32,1152]{1,0:T(8,128)(2,1)S(1)}, u32[]{:S(2)}, u32[]{:S(2)}) collective-permute-start(bf16[32,1152]{1,0:T(8,128)(2,1)S(1)} %copy-done.14), channel_id=1, source_target_pairs={{0,1},{1,0},{2,3},{3,2},{4,5},{5,4},{6,7},{7,6},{8,9},{9,8},{10,11... | collective-permute-start | bytes 221192 | tf_op jit(solution)/shard_map/ppermute | solution.py:45
  25.5 11.2 %collective-permute-start.8 = (bf16[32,1152]{1,0:T(8,128)(2,1)S(1)}, bf16[32,1152]{1,0:T(8,128)(2,1)S(1)}, u32[]{:S(2)}, u32[]{:S(2)}) collective-permute-start(bf16[32,1152]{1,0:T(8,128)(2,1)S(1)} %copy-done.14), channel_id=1, source_target_pairs={{0,2},{1,3},{2,0},{3,1},{4,6},{5,7},{6,4},{7,5},{8,10},{9,11},{10,... | collective-permute-start | bytes 221192 | tf_op jit(solution)/shard_map/ppermute | solution.py:45
  27.2 10.0 %collective-permute-start.9 = (bf16[32,1152]{1,0:T(8,128)(2,1)S(1)}, bf16[32,1152]{1,0:T(8,128)(2,1)S(1)}, u32[]{:S(2)}, u32[]{:S(2)}) collective-permute-start(bf16[32,1152]{1,0:T(8,128)(2,1)S(1)} %copy-done.14), channel_id=1, source_target_pairs={{0,3},{1,2},{2,1},{3,0},{4,7},{5,6},{6,5},{7,4},{8,11},{9,10},{10,... | collective-permute-start | bytes 221192 | tf_op jit(solution)/shard_map/ppermute | solution.py:45
  32.9 22.1 %collective-permute-start.10 = (bf16[3,32,1024]{2,1,0:T(8,128)(2,1)}, bf16[3,32,1024]{2,1,0:T(8,128)(2,1)S(1)}, u32[]{:S(2)}, u32[]{:S(2)}) collective-permute-start(bf16[3,32,1024]{2,1,0:T(8,128)(2,1)} %get-tuple-element.19), channel_id=1, source_target_pairs={{0,4},{4,0},{8,12},{12,8},{16,20},{20,16},{24,28},{28,24},{1,5},{5... | collective-permute-start | bytes 589832 | tf_op jit(solution)/shard_map/ppermute | solution.py:45
  33.4 23.9 %collective-permute-start.11 = (bf16[3,32,1024]{2,1,0:T(8,128)(2,1)}, bf16[3,32,1024]{2,1,0:T(8,128)(2,1)S(1)}, u32[]{:S(2)}, u32[]{:S(2)}) collective-permute-start(bf16[3,32,1024]{2,1,0:T(8,128)(2,1)} %get-tuple-element.20), channel_id=1, source_target_pairs={{0,8},{4,12},{8,0},{12,4},{16,24},{20,28},{24,16},{28,20},{1,9},{5... | collective-permute-start | bytes 589832 | tf_op jit(solution)/shard_map/ppermute | solution.py:45
  34.7 2.4 %copy-start.15 = (bf16[32,1152]{1,0:T(8,128)(2,1)}, bf16[32,1152]{1,0:T(8,128)(2,1)S(1)}, u32[]{:S(2)}) copy-start(bf16[32,1152]{1,0:T(8,128)(2,1)S(1)} %collective-permute-done.7.refs_1_) | copy-start | bytes 221188
  36.7 0.6 copy-start.16
  37.1 0.6 copy-start.17
  37.1 0.8 copy-start.8
  38.0 11.3 %copy-start.13 = (bf16[3,32,1024]{2,1,0:T(8,128)(2,1)S(1)}, bf16[3,32,1024]{2,1,0:T(8,128)(2,1)}, u32[]{:S(2)}) copy-start(bf16[3,32,1024]{2,1,0:T(8,128)(2,1)} %get-tuple-element.21) | copy-start | bytes 589828
  38.0 14.0 %copy-start.12 = (bf16[3,32,1024]{2,1,0:T(8,128)(2,1)S(1)}, bf16[3,32,1024]{2,1,0:T(8,128)(2,1)}, u32[]{:S(2)}) copy-start(bf16[3,32,1024]{2,1,0:T(8,128)(2,1)} %get-tuple-element.22) | copy-start | bytes 589828
  38.0 16.5 %copy-start.11 = (bf16[3,32,1024]{2,1,0:T(8,128)(2,1)S(1)}, bf16[3,32,1024]{2,1,0:T(8,128)(2,1)}, u32[]{:S(2)}) copy-start(bf16[3,32,1024]{2,1,0:T(8,128)(2,1)} %get-tuple-element.23) | copy-start | bytes 589828
  38.0 17.0 %copy-start.10 = (bf16[3,32,1024]{2,1,0:T(8,128)(2,1)S(1)}, bf16[3,32,1024]{2,1,0:T(8,128)(2,1)}, u32[]{:S(2)}) copy-start(bf16[3,32,1024]{2,1,0:T(8,128)(2,1)} %get-tuple-element.24) | copy-start | bytes 589828
  45.2 12.2 %copy-start.9 = (bf16[3,32,1024]{2,1,0:T(8,128)(2,1)S(1)}, bf16[3,32,1024]{2,1,0:T(8,128)(2,1)}, u32[]{:S(2)}) copy-start(bf16[3,32,1024]{2,1,0:T(8,128)(2,1)} %get-tuple-element.25) | copy-start | bytes 589828
  45.2 37.1 %all-to-all-start.1 = ((bf16[32,16,128]{2,1,0:T(8,128)(2,1)}), bf16[32,16,128]{2,1,0:T(8,128)(2,1)S(1)}, u32[]{:S(2)}, u32[]{:S(2)}) async-start(bf16[32,16,128]{2,1,0:T(8,128)(2,1)} %bitcast.18), calls=%async_computation.1 | async-start | bytes 262144 | tf_op jit(solution)/shard_map/all_to_all | solution.py:533
  49.3 14.6 %collective-permute-start.12 = (bf16[3,32,1024]{2,1,0:T(8,128)(2,1)S(1)}, bf16[3,32,1024]{2,1,0:T(8,128)(2,1)S(1)}, u32[]{:S(2)}, u32[]{:S(2)}) collective-permute-start(bf16[3,32,1024]{2,1,0:T(8,128)(2,1)S(1)} %copy-done.13), channel_id=1, source_target_pairs={{0,12},{4,8},{8,4},{12,0},{16,28},{20,24},{24,20},{28,16},{1,13},{... | collective-permute-start | bytes 589832 | tf_op jit(solution)/shard_map/ppermute | solution.py:45
  52.0 25.6 %collective-permute-start.13 = (bf16[3,32,1024]{2,1,0:T(8,128)(2,1)S(1)}, bf16[3,32,1024]{2,1,0:T(8,128)(2,1)S(1)}, u32[]{:S(2)}, u32[]{:S(2)}) collective-permute-start(bf16[3,32,1024]{2,1,0:T(8,128)(2,1)S(1)} %copy-done.12), channel_id=1, source_target_pairs={{0,16},{4,20},{8,24},{12,28},{16,0},{20,4},{24,8},{28,12},{1,17},{... | collective-permute-start | bytes 589832 | tf_op jit(solution)/shard_map/ppermute | solution.py:45
  54.4 27.8 %collective-permute-start.14 = (bf16[3,32,1024]{2,1,0:T(8,128)(2,1)S(1)}, bf16[3,32,1024]{2,1,0:T(8,128)(2,1)S(1)}, u32[]{:S(2)}, u32[]{:S(2)}) collective-permute-start(bf16[3,32,1024]{2,1,0:T(8,128)(2,1)S(1)} %copy-done.11), channel_id=1, source_target_pairs={{0,20},{4,16},{8,28},{12,24},{16,4},{20,0},{24,12},{28,8},{1,21},{... | collective-permute-start | bytes 589832 | tf_op jit(solution)/shard_map/ppermute | solution.py:45
  54.9 27.3 %collective-permute-start.15 = (bf16[3,32,1024]{2,1,0:T(8,128)(2,1)S(1)}, bf16[3,32,1024]{2,1,0:T(8,128)(2,1)S(1)}, u32[]{:S(2)}, u32[]{:S(2)}) collective-permute-start(bf16[3,32,1024]{2,1,0:T(8,128)(2,1)S(1)} %copy-done.10), channel_id=1, source_target_pairs={{0,24},{4,28},{8,16},{12,20},{16,8},{20,12},{24,0},{28,4},{1,25},{... | collective-permute-start | bytes 589832 | tf_op jit(solution)/shard_map/ppermute | solution.py:45
  57.3 25.0 %copy-start.7 = (bf16[3,32,1024]{2,1,0:T(8,128)(2,1)S(1)}, bf16[3,32,1024]{2,1,0:T(8,128)(2,1)}, u32[]{:S(2)}) copy-start(bf16[3,32,1024]{2,1,0:T(8,128)(2,1)} %get-tuple-element.18.refs_0_) | copy-start | bytes 589828
  57.3 24.9 %collective-permute-start.16 = (bf16[3,32,1024]{2,1,0:T(8,128)(2,1)S(1)}, bf16[3,32,1024]{2,1,0:T(8,128)(2,1)S(1)}, u32[]{:S(2)}, u32[]{:S(2)}) collective-permute-start(bf16[3,32,1024]{2,1,0:T(8,128)(2,1)S(1)} %copy-done.9), channel_id=1, source_target_pairs={{0,28},{4,24},{8,20},{12,16},{16,12},{20,8},{24,4},{28,0},{1,29},{... | collective-permute-start | bytes 589832 | tf_op jit(solution)/shard_map/ppermute | solution.py:45
  89.3 24.5 %all-to-all-start.2 = ((bf16[8,32,1024]{2,1,0:T(8,128)(2,1)}), bf16[8,32,1024]{2,1,0:T(8,128)(2,1)S(1)}, u32[]{:S(2)}, u32[]{:S(2)}) async-start(bf16[8,32,1024]{2,1,0:T(8,128)(2,1)} %attention.1), calls=%async_computation.2 | async-start | bytes 1048576 | tf_op jit(solution)/shard_map/all_to_all | solution.py:565
  101.8 12.0 %copy-start.1 = (bf16[32,32,256]{2,1,0:T(8,128)(2,1)S(1)}, bf16[32,32,256]{2,1,0:T(8,128)(2,1)}, u32[]{:S(2)}) copy-start(bf16[32,32,256]{2,1,0:T(8,128)(2,1)} %x_ref.1) | copy-start | bytes 1572868
  101.8 12.0 %copy-start.2 = (bf16[256,1024]{1,0:T(8,128)(2,1)S(1)}, bf16[256,1024]{1,0:T(8,128)(2,1)}, u32[]{:S(2)}) copy-start(bf16[256,1024]{1,0:T(8,128)(2,1)} %up_ref.1) | copy-start | bytes 1572868
  101.8 12.0 %copy-start.3 = (bf16[1024,256]{1,0:T(8,128)(2,1)S(1)}, bf16[1024,256]{1,0:T(8,128)(2,1)}, u32[]{:S(2)}) copy-start(bf16[1024,256]{1,0:T(8,128)(2,1)} %down_ref.1) | copy-start | bytes 1572868
  105.3 8.5 %copy-start.4 = (f32[256]{0:T(256)S(1)}, f32[256]{0:T(256)}, u32[]{:S(2)}) copy-start(f32[256]{0:T(256)} %param.35) | copy-start | bytes 3076
  113.9 1.2 %copy-start.5 = (f32[8,32,1024]{2,1,0:T(8,128)S(1)}, f32[8,32,1024]{2,1,0:T(8,128)}, u32[]{:S(2)}) copy-start(f32[8,32,1024]{2,1,0:T(8,128)} %gates.1.gate_ref) | copy-start | bytes 3145732
  115.1 1.0 copy-start.6
